TPU v7x, 1024 devices: a whole 4x8x16 slice. The times are simulated.
1024 devices in a mesh: grp: 8 (over x, y_lo), sub: 128 (over z, y_hi, core).
Axes of the slice: x: 4, y: 8 (y_hi: 4, y_lo: 2; y = y_hi * 2 + y_lo), z: 16, core: 2. Of those that a mesh axis runs over, the one named last changes fastest.
Arguments:
- reg_disp: float32 [8, 128, 3, 384], P('grp', 'sub'), may hold values from -6 to 6
- reg_vel: float32 [8, 128, 3, 384], P('grp', 'sub'), may hold values from -0.6 to 0.6
- site_disp: float32 [8, 128, 3, 1536], P('grp', 'sub'), may hold values from -6 to 6
- site_vel: float32 [8, 128, 3, 1536], P('grp', 'sub'), may hold values from -0.6 to 0.6
- reg_nodes: int32 [8, 128, 10, 256], P('grp', 'sub'), may hold values from 0 to 383
- site_nodes: int32 [8, 128, 35, 128], P('grp', 'sub'), may hold values from 0 to 1535
- reg_coefs: float32 [8, 128, 3, 3, 4, 256], P('grp', 'sub'), may hold values from -1.5 to 6, as said below
- site_coefs: float32 [8, 128, 3, 3, 24, 128], P('grp', 'sub'), may hold values from -1.5 to 6, as said below
- reg_table: float32 [12, 10], replicated, may hold values from -2 to 2
- site_table: float32 [72, 35], replicated, may hold values from -1 to 1
- reg_minv: float32 [8, 128, 384], P('grp', 'sub'), may hold values from 0.003 to 0.015
- site_minv: float32 [8, 128, 1536], P('grp', 'sub'), may hold values from 0.003 to 0.015
- reg_send: int32 [8, 128, 2, 128], P('grp', 'sub'), may hold values from 0 to 383
- reg_recv: int32 [8, 128, 2, 128], P('grp', 'sub'), may hold values from 0 to 383
- site_send: int32 [8, 128, 2, 128], P('grp', 'sub'), may hold values from 0 to 1535
- site_recv: int32 [8, 128, 2, 128], P('grp', 'sub'), may hold values from 0 to 1535
- slot_fill: int32 [8, 128, 4], P('grp', 'sub'), may hold values from 1 to 128, 384 in all within a row
- layer_src: int32 [8, 128, 128], P('grp', 'sub'), may hold values from 0 to 383
- layer_fill: int32 [8, 128], P('grp', 'sub'), may hold values from 64 to 128, as said below
- layer_dst: int32 [8, 128, 3, 128], P('grp', 'sub'), may hold values from 0 to 1535
- layer_stiff: float32 [8, 128, 3, 128], P('grp', 'sub'), may hold values from 0.5 to 2
Outputs:
- reg_final: float32 [8, 128, 3, 384], P('grp', 'sub')
- site_final: float32 [8, 128, 3, 1536], P('grp', 'sub')
Inputs may be any that keep to these rules, and one draw needn't show every extreme that they name: `slot_fill`: per partition the four entries count live slots toward the lower and higher neighbour, regional then site; they sum to 384. `layer_fill`: partition index 0 of every group fills all 128 slots. `reg_coefs`: each 3 x 3 tensor over the first two dimensions is symmetric positive definite. `site_coefs`: each 3 x 3 tensor over the first two dimensions is symmetric positive definite.
All inputs are finite; a program needn't handle non-finite values.
Results may differ from a plain program's by a relative error of at most 0.0003.
Values sent between devices are 32-bit elements; how exact they have to be, the bound alone decides.
A program may use at most 64 MiB of HBM per device.

v0:
```python
import jax
import jax.numpy as jnp
from jax import lax
from jax.sharding import PartitionSpec as P

STEPS = 8
MB_STEPS = 2


PRECISE = lax.Precision.HIGHEST


def with_halo(value, sides, width):
    for axis, dim in sides:
        count, length = (lax.axis_size(axis), value.shape[dim])
        up = [(i, (i + 1) % count) for i in range(count - 1)]
        down = [(j, i) for i, j in up]
        last = lax.slice_in_dim(value, length - width, length, axis=dim)
        leading = lax.slice_in_dim(value, 0, width, axis=dim)
        before = lax.ppermute(last, axis, up)
        after = lax.ppermute(leading, axis, down)
        value = jnp.concatenate([before, value, after], axis=dim)
    return value


def shifted(block, axis, distance):
    devices = range(lax.axis_size(axis))
    route = [(i - distance, i) for i in devices if i - distance in devices]
    return lax.ppermute(block, axis, route)


def stiff_force(displaced, element_nodes, coef_block, deriv_table):
    quad_count = coef_block.shape[2]
    node_count = element_nodes.shape[0]
    elem_count = element_nodes.shape[1]
    flat_nodes = element_nodes.reshape(-1)
    gathered = jnp.take(displaced, flat_nodes, axis=1).reshape(3, node_count, elem_count)
    gradient = jnp.einsum("kp,cpe->cke", deriv_table, gathered, precision=PRECISE)
    pieces = [gradient[:, b * quad_count : (b + 1) * quad_count] for b in range(3)]
    flux_rows = [
        coef_block[a, 0][None] * pieces[0]
        + coef_block[a, 1][None] * pieces[1]
        + coef_block[a, 2][None] * pieces[2]
        for a in range(3)
    ]
    flux_terms = jnp.concatenate(flux_rows, axis=1)
    element_terms = jnp.einsum("kp,cke->cpe", deriv_table, flux_terms, precision=PRECISE)
    return -jnp.zeros_like(displaced).at[:, flat_nodes].add(element_terms.reshape(3, -1))


def pack_slots(forces, send_map, fill_pair):
    picked = jnp.take(forces, send_map, axis=1)
    live_slots = jnp.arange(send_map.shape[1], dtype=jnp.int32)[None, :] < fill_pair[:, None]
    return jnp.where(live_slots[:, None, :], jnp.transpose(picked, (1, 0, 2)), 0.0)


def take_slots(forces, recv_map, from_lower, from_upper):
    return forces.at[:, recv_map[0]].add(from_lower).at[:, recv_map[1]].add(from_upper)


def pack_layer(displaced, layer_src, layer_fill):
    picked = jnp.take(displaced, layer_src, axis=1)
    live_slots = jnp.arange(layer_src.shape[0], dtype=jnp.int32) < layer_fill
    return jnp.where(live_slots[None, :], picked, 0.0)


def add_layer(forces, layer_dst, layer_stiff, layer_block):
    for source in range(3):
        forces = forces.at[:, layer_dst[source]].add(
            layer_stiff[source][None, :] * layer_block[source]
        )
    return forces


def shards(
    reg_disp,
    reg_vel,
    site_disp,
    site_vel,
    reg_nodes,
    site_nodes,
    reg_coefs,
    site_coefs,
    reg_table,
    site_table,
    reg_minv,
    site_minv,
    reg_send,
    reg_recv,
    site_send,
    site_recv,
    slot_fill,
    layer_src,
    layer_fill,
    layer_dst,
    layer_stiff,
):
    group_count = lax.axis_size("grp")
    site_groups = group_count // 4
    reg_groups = 3 * site_groups
    grp_index = lax.axis_index("grp")
    is_site = grp_index >= reg_groups
    reg_now = reg_disp[0, 0]
    site_now = site_disp[0, 0]
    slot_counts = slot_fill[0, 0]
    blank_send = jnp.zeros((2, 3, reg_send.shape[-1]), jnp.float32)

    def advance(states, layer_block, reg_on, site_on):
        reg_pair, site_pair = states

        def reg_force():
            forces = stiff_force(reg_pair[1], reg_nodes[0, 0], reg_coefs[0, 0], reg_table)
            return (
                forces,
                jnp.zeros_like(site_pair[1]),
                pack_slots(forces, reg_send[0, 0], slot_counts[0:2]),
            )

        def site_force():
            forces = stiff_force(site_pair[1], site_nodes[0, 0], site_coefs[0, 0], site_table)
            return (
                jnp.zeros_like(reg_pair[1]),
                forces,
                pack_slots(forces, site_send[0, 0], slot_counts[2:4]),
            )

        def no_force():
            return (jnp.zeros_like(reg_pair[1]), jnp.zeros_like(site_pair[1]), blank_send)

        reg_total, site_total, outgoing = lax.cond(
            is_site, site_force if site_on else no_force, reg_force if reg_on else no_force
        )
        incoming = with_halo(outgoing, (("sub", 0),), 1)
        from_lower = incoming[0]
        from_upper = incoming[3]

        def reg_update():
            forces = take_slots(reg_total, reg_recv[0, 0], from_lower, from_upper)
            reg_next = 2.0 * reg_pair[1] - reg_pair[0] + reg_minv[0, 0][None, :] * forces
            return ((reg_pair[1], reg_next), site_pair)

        def site_update():
            forces = take_slots(site_total, site_recv[0, 0], from_lower, from_upper)
            forces = add_layer(forces, layer_dst[0, 0], layer_stiff[0, 0], layer_block)
            site_next = 2.0 * site_pair[1] - site_pair[0] + site_minv[0, 0][None, :] * forces
            return (reg_pair, (site_pair[1], site_next))

        def keep_states():
            return (reg_pair, site_pair)

        return lax.cond(
            is_site, site_update if site_on else keep_states, reg_update if reg_on else keep_states
        )

    states = ((reg_now - reg_vel[0, 0], reg_now), (site_now - site_vel[0, 0], site_now))
    batch_count = STEPS // MB_STEPS
    pending = None
    for batch_no in range(batch_count + 1):
        layer_packs = []
        for inner_step in range(MB_STEPS):
            layer_block = pending[:, inner_step] if batch_no > 0 else None
            states = advance(states, layer_block, batch_no < batch_count, batch_no > 0)
            if batch_no < batch_count:
                layer_packs.append(pack_layer(states[0][1], layer_src[0, 0], layer_fill[0, 0]))
        if batch_no < batch_count:
            layer_steps = jnp.stack(layer_packs)
            pending = jnp.stack(
                [shifted(layer_steps, "grp", (3 - source) * site_groups) for source in range(3)]
            )
    reg_final = jnp.where(is_site, 0.0, states[0][1])[None, None]
    site_final = jnp.where(is_site, states[1][1], 0.0)[None, None]
    return (reg_final, site_final)


def solution(mesh):
    return jax.shard_map(
        shards,
        mesh=mesh,
        in_specs=(
            P("grp", "sub", None, None),
            P("grp", "sub", None, None),
            P("grp", "sub", None, None),
            P("grp", "sub", None, None),
            P("grp", "sub", None, None),
            P("grp", "sub", None, None),
            P("grp", "sub", None, None, None, None),
            P("grp", "sub", None, None, None, None),
            P(),
            P(),
            P("grp", "sub", None),
            P("grp", "sub", None),
            P("grp", "sub", None, None),
            P("grp", "sub", None, None),
            P("grp", "sub", None, None),
            P("grp", "sub", None, None),
            P("grp", "sub", None),
            P("grp", "sub", None),
            P("grp", "sub"),
            P("grp", "sub", None, None),
            P("grp", "sub", None, None),
        ),
        out_specs=(P("grp", "sub", None, None), P("grp", "sub", None, None)),
        check_vma=False,
    )
```

profile of v0, /device:TPU:255, one launch (start us, length us, event | category | flops | bytes accessed | tf_op | source)
XLA Modules:
  0.0 631.4 jit_solution(4486505092661364522)
XLA Ops:
  35.3 47.2 %conditional.24 = (f32[3,384]{0,1:T(8,128)S(1)}, f32[3,1536]{1,0:T(4,128)S(1)}, f32[2,3,128]{1,2,0:T(8,128)}) conditional(s32[]{:T(128)} %convert_element_type.2, (s32[1,1,10,256]{3,1,2,0:T(1,128)S(1)}, f32[1,1,3,3,4,256]{5,4,3,2,1,0:T(4,128)S(1)}, f32[3,384]{0,1:T(8,128)S(1)}, f32[12,10]{1,0:T(8,128)S(1)}, s32[4]{0:T(128)S(1)}, ...), branch_computations={%region_14.18_spmd, %region_16.22_spmd} | conditional | flops 23513344 | bytes 1754184 | solution.py:130
  36.0 9.2 %gather_fusion.6 = f32[4480,3]{1,0:T(8,128)} fusion(f32[3,1536]{0,1:T(8,128)S(1)} %get-tuple-element.568, s32[5120]{0:T(1024)S(1)} %pad_clamp_fusion.6), kind=kCustom, calls=%fused_computation.2.clone | custom fusion | bytes 125440 | tf_op jit(solution)/shard_map/cond/branch_1_fun/jit(_take)/gather | solution.py:37
  54.8 25.6 %scatter_custom_fusion.5 = f32[3,1536]{0,1:T(8,128)S(1)} fusion(s32[4480]{0:T(1024)S(1)} %fusion.289, f32[4480,3]{1,0:T(8,128)} %bitcast.1637, f32[]{:T(128)} %constant.72.clone), kind=kCustom, calls=%fused_computation.562 | custom fusion | flops 13440 | bytes 18944 | tf_op jit(solution)/shard_map/cond/branch_1_fun/scatter-add | solution.py:48
  96.9 12.6 %conditional.25 = (f32[3,384]{1,0:T(4,128)S(1)}, f32[3,384]{1,0:T(4,128)S(1)}, f32[3,1536]{0,1:T(8,128)S(1)}, f32[3,1536]{0,1:T(8,128)S(1)}, f32[3,384]{0,1:T(8,128)S(1)}) conditional(s32[]{:T(128)} %convert_element_type.2, (f32[3,384]{0,1:T(8,128)S(1)}, f32[3,384]{0,1:T(8,128)S(1)}, f32[1,1,384]{2,1,0:T(1,128)S(1)}, ...), branch_computations={%region_18.0_spmd, %region_21.32_spmd} | conditional | flops 23424 | bytes 712264 | solution.py:151
  110.4 47.2 %conditional.26 = (f32[3,384]{0,1:T(8,128)S(1)}, f32[3,1536]{1,0:T(4,128)S(1)}, f32[2,3,128]{1,2,0:T(8,128)}) conditional(s32[]{:T(128)} %convert_element_type.2, (s32[1,1,10,256]{3,1,2,0:T(1,128)S(1)}, f32[1,1,3,3,4,256]{5,4,3,2,1,0:T(4,128)S(1)}, f32[3,384]{1,0:T(4,128)S(1)}, f32[12,10]{1,0:T(8,128)S(1)}, s32[4]{0:T(128)}, ...), branch_computations={%region_27.34_spmd, %region_29.36_spmd} | conditional | flops 23513344 | bytes 1705096 | solution.py:130
  111.1 9.2 %gather_fusion.10 = f32[4480,3]{1,0:T(8,128)} fusion(f32[3,1536]{0,1:T(8,128)S(1)} %get-tuple-element.601, s32[5120]{0:T(1024)S(1)} %pad_clamp_fusion.10), kind=kCustom, calls=%fused_computation.19.clone | custom fusion | bytes 125440 | tf_op jit(solution)/shard_map/cond/branch_1_fun/jit(_take)/gather | solution.py:37
  130.0 25.6 %scatter_custom_fusion.65 = f32[3,1536]{0,1:T(8,128)S(1)} fusion(s32[4480]{0:T(1024)S(1)} %fusion.315, f32[4480,3]{1,0:T(8,128)} %bitcast.1638, f32[]{:T(128)} %constant.104.clone), kind=kCustom, calls=%fused_computation.636 | custom fusion | flops 13440 | bytes 18944 | tf_op jit(solution)/shard_map/cond/branch_1_fun/scatter-add | solution.py:48
  170.8 11.4 %conditional.27 = (f32[3,384]{1,0:T(4,128)S(1)}, f32[3,384]{1,0:T(4,128)S(1)}, f32[3,1536]{0,1:T(8,128)S(1)}, f32[3,1536]{0,1:T(8,128)S(1)}, f32[3,384]{0,1:T(8,128)S(1)}) conditional(s32[]{:T(128)} %convert_element_type.2, (f32[3,384]{1,0:T(4,128)S(1)}, f32[3,384]{1,0:T(4,128)S(1)}, f32[1,1,384]{2,1,0:T(1,128)S(1)}, s32[1,1,2,128]{3,2,1,0:T(2,128)}, ...), branch_computations={%region_31.39_spmd, %region_34.45_spmd} | conditional | flops 23424 | bytes 739940 | solution.py:151
  188.6 44.3 %conditional.28 = (f32[3,384]{0,1:T(8,128)S(1)}, f32[3,1536]{1,0:T(4,128)S(1)}, f32[2,3,128]{1,2,0:T(8,128)}) conditional(s32[]{:T(128)} %convert_element_type.2, (s32[1,1,10,256]{3,1,2,0:T(1,128)S(1)}, f32[1,1,3,3,4,256]{5,4,3,2,1,0:T(4,128)S(1)}, f32[3,384]{1,0:T(4,128)S(1)}, f32[12,10]{1,0:T(8,128)S(1)}, s32[4]{0:T(128)}, ...), branch_computations={%region_40.47_spmd, %region_42.49_spmd} | conditional | flops 23513344 | bytes 1606736 | solution.py:130
  188.6 9.2 %gather_fusion.14 = f32[4480,3]{1,0:T(8,128)} fusion(f32[3,1536]{0,1:T(8,128)S(1)} %get-tuple-element.634, s32[5120]{0:T(1024)S(1)} %pad_clamp_fusion.14), kind=kCustom, calls=%fused_computation.20.clone | custom fusion | bytes 125440 | tf_op jit(solution)/shard_map/cond/branch_1_fun/jit(_take)/gather | solution.py:37
  205.2 25.6 %scatter_custom_fusion.66 = f32[3,1536]{0,1:T(8,128)S(1)} fusion(s32[4480]{0:T(1024)S(1)} %fusion.341, f32[4480,3]{1,0:T(8,128)} %bitcast.1639, f32[]{:T(128)} %constant.128.clone), kind=kCustom, calls=%fused_computation.710 | custom fusion | flops 13440 | bytes 18944 | tf_op jit(solution)/shard_map/cond/branch_1_fun/scatter-add | solution.py:48
  246.8 11.3 %conditional.29 = (f32[3,384]{1,0:T(4,128)S(1)}, f32[3,384]{1,0:T(4,128)S(1)}, f32[3,1536]{0,1:T(8,128)S(1)}, f32[3,1536]{0,1:T(8,128)S(1)}, f32[3,384]{0,1:T(8,128)S(1)}) conditional(s32[]{:T(128)} %convert_element_type.2, (f32[3,384]{1,0:T(4,128)S(1)}, f32[3,384]{1,0:T(4,128)S(1)}, f32[1,1,384]{2,1,0:T(1,128)S(1)}, s32[1,1,2,128]{3,2,1,0:T(2,128)}, ...), branch_computations={%region_44.52_spmd, %region_47.58_spmd} | conditional | flops 23424 | bytes 624284 | solution.py:151
  259.1 44.3 %conditional.30 = (f32[3,384]{0,1:T(8,128)S(1)}, f32[3,1536]{1,0:T(4,128)S(1)}, f32[2,3,128]{1,2,0:T(8,128)}) conditional(s32[]{:T(128)} %convert_element_type.2, (s32[1,1,10,256]{3,1,2,0:T(1,128)S(1)}, f32[1,1,3,3,4,256]{5,4,3,2,1,0:T(4,128)S(1)}, f32[3,384]{1,0:T(4,128)S(1)}, f32[12,10]{1,0:T(8,128)S(1)}, s32[4]{0:T(128)}, ...), branch_computations={%region_53.60_spmd, %region_55.62_spmd} | conditional | flops 23513344 | bytes 1606736 | solution.py:130
  259.1 9.2 %gather_fusion.18 = f32[4480,3]{1,0:T(8,128)} fusion(f32[3,1536]{0,1:T(8,128)S(1)} %get-tuple-element.667, s32[5120]{0:T(1024)S(1)} %pad_clamp_fusion.18), kind=kCustom, calls=%fused_computation.21.clone | custom fusion | bytes 125440 | tf_op jit(solution)/shard_map/cond/branch_1_fun/jit(_take)/gather | solution.py:37
  275.7 25.6 %scatter_custom_fusion.67 = f32[3,1536]{0,1:T(8,128)S(1)} fusion(s32[4480]{0:T(1024)S(1)} %fusion.367, f32[4480,3]{1,0:T(8,128)} %bitcast.1640, f32[]{:T(128)} %constant.152.clone), kind=kCustom, calls=%fused_computation.784 | custom fusion | flops 13440 | bytes 18944 | tf_op jit(solution)/shard_map/cond/branch_1_fun/scatter-add | solution.py:48
  316.0 11.4 %conditional.31 = (f32[3,384]{1,0:T(4,128)S(1)}, f32[3,384]{1,0:T(4,128)S(1)}, f32[3,1536]{0,1:T(8,128)S(1)}, f32[3,1536]{0,1:T(8,128)S(1)}, f32[3,384]{0,1:T(8,128)S(1)}) conditional(s32[]{:T(128)} %convert_element_type.2, (f32[3,384]{1,0:T(4,128)S(1)}, f32[3,384]{1,0:T(4,128)S(1)}, f32[1,1,384]{2,1,0:T(1,128)S(1)}, s32[1,1,2,128]{3,2,1,0:T(2,128)}, ...), branch_computations={%region_57.65_spmd, %region_60.71_spmd} | conditional | flops 23424 | bytes 739940 | solution.py:151
  333.8 44.3 %conditional.32 = (f32[3,384]{0,1:T(8,128)S(1)}, f32[3,1536]{1,0:T(4,128)S(1)}, f32[2,3,128]{1,2,0:T(8,128)}) conditional(s32[]{:T(128)} %convert_element_type.2, (s32[1,1,10,256]{3,1,2,0:T(1,128)S(1)}, f32[1,1,3,3,4,256]{5,4,3,2,1,0:T(4,128)S(1)}, f32[3,384]{1,0:T(4,128)S(1)}, f32[12,10]{1,0:T(8,128)S(1)}, s32[4]{0:T(128)}, ...), branch_computations={%region_66.73_spmd, %region_68.75_spmd} | conditional | flops 23513344 | bytes 1606736 | solution.py:130
  333.9 9.2 %gather_fusion.22 = f32[4480,3]{1,0:T(8,128)} fusion(f32[3,1536]{0,1:T(8,128)S(1)} %get-tuple-element.700, s32[5120]{0:T(1024)S(1)} %pad_clamp_fusion.22), kind=kCustom, calls=%fused_computation.22.clone | custom fusion | bytes 125440 | tf_op jit(solution)/shard_map/cond/branch_1_fun/jit(_take)/gather | solution.py:37
  350.5 25.6 %scatter_custom_fusion.68 = f32[3,1536]{0,1:T(8,128)S(1)} fusion(s32[4480]{0:T(1024)S(1)} %fusion.393, f32[4480,3]{1,0:T(8,128)} %bitcast.1641, f32[]{:T(128)} %constant.176.clone), kind=kCustom, calls=%fused_computation.858 | custom fusion | flops 13440 | bytes 18944 | tf_op jit(solution)/shard_map/cond/branch_1_fun/scatter-add | solution.py:48
  392.4 10.7 %conditional.33 = (f32[3,384]{1,0:T(4,128)S(1)}, f32[3,384]{1,0:T(4,128)S(1)}, f32[3,1536]{0,1:T(8,128)S(1)}, f32[3,1536]{0,1:T(8,128)S(1)}, f32[3,384]{0,1:T(8,128)S(1)}) conditional(s32[]{:T(128)} %convert_element_type.2, (f32[3,384]{1,0:T(4,128)S(1)}, f32[3,384]{1,0:T(4,128)S(1)}, f32[1,1,384]{2,1,0:T(1,128)S(1)}, s32[1,1,2,128]{3,2,1,0:T(2,128)}, ...), branch_computations={%region_70.78_spmd, %region_73.84_spmd} | conditional | flops 23424 | bytes 739940 | solution.py:151
  404.1 44.3 %conditional.34 = (f32[3,384]{0,1:T(8,128)S(1)}, f32[3,1536]{1,0:T(4,128)S(1)}, f32[2,3,128]{1,2,0:T(8,128)}) conditional(s32[]{:T(128)} %convert_element_type.2, (s32[1,1,10,256]{3,1,2,0:T(1,128)S(1)}, f32[1,1,3,3,4,256]{5,4,3,2,1,0:T(4,128)S(1)}, f32[3,384]{1,0:T(4,128)S(1)}, f32[12,10]{1,0:T(8,128)S(1)}, s32[4]{0:T(128)}, ...), branch_computations={%region_79.86_spmd, %region_81.88_spmd} | conditional | flops 23513344 | bytes 1606736 | solution.py:130
  404.1 9.2 %gather_fusion.26 = f32[4480,3]{1,0:T(8,128)} fusion(f32[3,1536]{0,1:T(8,128)S(1)} %get-tuple-element.733, s32[5120]{0:T(1024)S(1)} %pad_clamp_fusion.26), kind=kCustom, calls=%fused_computation.23.clone | custom fusion | bytes 125440 | tf_op jit(solution)/shard_map/cond/branch_1_fun/jit(_take)/gather | solution.py:37
  420.7 25.6 %scatter_custom_fusion.69 = f32[3,1536]{0,1:T(8,128)S(1)} fusion(s32[4480]{0:T(1024)S(1)} %fusion.419, f32[4480,3]{1,0:T(8,128)} %bitcast.1642, f32[]{:T(128)} %constant.200.clone), kind=kCustom, calls=%fused_computation.932 | custom fusion | flops 13440 | bytes 18944 | tf_op jit(solution)/shard_map/cond/branch_1_fun/scatter-add | solution.py:48
  461.0 10.5 %conditional.35 = (f32[3,384]{1,0:T(4,128)S(1)}, f32[3,1536]{0,1:T(8,128)S(1)}, f32[3,1536]{0,1:T(8,128)S(1)}, f32[3,384]{0,1:T(8,128)S(1)}) conditional(s32[]{:T(128)} %convert_element_type.2, (f32[3,384]{1,0:T(4,128)S(1)}, f32[3,384]{1,0:T(4,128)S(1)}, f32[1,1,384]{2,1,0:T(1,128)S(1)}, s32[1,1,2,128]{3,2,1,0:T(2,128)}, f32[3,384]{0,1:T(8,128)S(1)}, ...), branch_computations={%region_83.91_spmd, %region_86.97_spmd} | conditional | flops 23424 | bytes 739932 | solution.py:151
  477.9 45.4 %conditional.36 = (f32[3,1536]{0,1:T(8,128)}, f32[2,3,128]{1,2,0:T(8,128)S(1)}) conditional(s32[]{:T(128)} %convert_element_type.2, () %tuple.204, (s32[1,1,35,128]{3,1,2,0:T(1,128)S(1)}, f32[1,1,3,3,24,128]{5,4,3,2,1,0:T(8,128)S(1)}, f32[3,1536]{0,1:T(8,128)S(1)}, f32[72,35]{0,1:T(8,128)S(1)}, s32[4]{0:T(128)S(1)}, ...), branch_computations={%region_92.98_spmd, %region_93.100_spmd} | conditional | flops 23513344 | bytes 1565160 | solution.py:130
  478.0 9.2 %gather_fusion.28 = f32[4480,3]{1,0:T(8,128)} fusion(f32[3,1536]{0,1:T(8,128)S(1)} %get-tuple-element.759, s32[5120]{0:T(1024)S(1)} %pad_clamp_fusion.28), kind=kCustom, calls=%fused_computation.24.clone | custom fusion | bytes 125440 | tf_op jit(solution)/shard_map/cond/branch_1_fun/jit(_take)/gather | solution.py:37
  494.6 25.6 %scatter_custom_fusion.70 = f32[3,1536]{0,1:T(8,128)S(1)} fusion(s32[4480]{0:T(1024)S(1)} %fusion.432, f32[4480,3]{1,0:T(8,128)} %bitcast.1635, f32[]{:T(128)} %constant.209.clone), kind=kCustom, calls=%fused_computation.969 | custom fusion | flops 13440 | bytes 18944 | tf_op jit(solution)/shard_map/cond/branch_1_fun/scatter-add | solution.py:48
  535.5 17.9 %conditional.37 = (f32[3,1536]{0,1:T(8,128)S(1)}, f32[3,1536]{0,1:T(8,128)S(1)}) conditional(s32[]{:T(128)} %convert_element_type.2, (f32[3,1536]{0,1:T(8,128)}, f32[3,1536]{0,1:T(8,128)S(1)}) %tuple.663, (f32[3,1536]{0,1:T(8,128)S(1)}, f32[3,1536]{0,1:T(8,128)}, f32[1,1,1536]{2,1,0:T(1,128)S(1)}, s32[1,1,2,128]{3,2,1,0:T(2,128)S(1)}, ...), branch_computations={%region_95.101_spmd.clone, %region_96.0_spmd.clone} | conditional | flops 23424 | bytes 656944 | solution.py:151
  554.3 46.0 %conditional.38 = (f32[3,1536]{0,1:T(8,128)}, f32[2,3,128]{1,2,0:T(8,128)S(1)}) conditional(s32[]{:T(128)} %convert_element_type.2, () %tuple.207, (s32[1,1,35,128]{3,1,2,0:T(1,128)S(1)}, f32[1,1,3,3,24,128]{5,4,3,2,1,0:T(8,128)S(1)}, f32[3,1536]{0,1:T(8,128)S(1)}, f32[72,35]{0,1:T(8,128)S(1)}, s32[4]{0:T(128)S(1)}, ...), branch_computations={%region_102.108_spmd, %region_103.110_spmd} | conditional | flops 23513344 | bytes 1565160 | solution.py:130
  554.6 9.2 %gather_fusion.30 = f32[4480,3]{1,0:T(8,128)} fusion(f32[3,1536]{0,1:T(8,128)S(1)} %get-tuple-element.777, s32[5120]{0:T(1024)S(1)} %pad_clamp_fusion.30), kind=kCustom, calls=%fused_computation.25.clone | custom fusion | bytes 125440 | tf_op jit(solution)/shard_map/cond/branch_1_fun/jit(_take)/gather | solution.py:37
  571.2 25.6 %scatter_custom_fusion.71 = f32[3,1536]{0,1:T(8,128)S(1)} fusion(s32[4480]{0:T(1024)S(1)} %fusion.445, f32[4480,3]{1,0:T(8,128)} %bitcast.1636, f32[]{:T(128)} %constant.223.clone), kind=kCustom, calls=%fused_computation.1006 | custom fusion | flops 13440 | bytes 18944 | tf_op jit(solution)/shard_map/cond/branch_1_fun/scatter-add | solution.py:48
  612.0 18.2 %conditional.39 = (f32[3,1536]{1,0:T(4,128)S(1)}) conditional(s32[]{:T(128)} %convert_element_type.2, f32[3,1536]{0,1:T(8,128)S(1)} %get-tuple-element.900, (f32[3,1536]{0,1:T(8,128)S(1)}, f32[3,1536]{0,1:T(8,128)}, f32[1,1,1536]{2,1,0:T(1,128)S(1)}, s32[1,1,2,128]{3,2,1,0:T(2,128)S(1)}, f32[3,1536]{0,1:T(8,128)}, ...), branch_computations={%region_105.111_spmd, %region_106.0_spmd} | conditional | flops 23424 | bytes 656936 | solution.py:151
  (534 shorter events, 343.9 us)
Async XLA Ops:
  1.7 9.4 %collective-permute-start = (f32[1,3,128]{1,2,0:T(8,128)S(1)}, f32[1,3,128]{1,2,0:T(8,128)S(1)}, u32[]{:S(2)}, u32[]{:S(2)}) collective-permute-start(f32[1,3,128]{1,2,0:T(8,128)S(1)} %get-tuple-element.2092), channel_id=1, source_target_pairs={{0,1},{1,2},{2,3},{3,4},{4,5},{5,6},{6,7},{7,8},{8,9},{9,10},{10,1... | collective-permute-start | bytes 4616 | tf_op jit(solution)/shard_map/ppermute | solution.py:20
  7.6 9.8 %collective-permute-start.1 = (f32[1,3,128]{1,2,0:T(8,128)S(1)}, f32[1,3,128]{1,2,0:T(8,128)S(1)}, u32[]{:S(2)}, u32[]{:S(2)}) collective-permute-start(f32[1,3,128]{1,2,0:T(8,128)S(1)} %get-tuple-element.2091), channel_id=1, source_target_pairs={{1,0},{2,1},{3,2},{4,3},{5,4},{6,5},{7,6},{8,7},{9,8},{10,9},{11,1... | collective-permute-start | bytes 4616 | tf_op jit(solution)/shard_map/ppermute | solution.py:21
  17.7 6.7 %collective-permute-start.2 = (f32[1,3,128]{1,2,0:T(8,128)S(1)}, f32[1,3,128]{1,2,0:T(8,128)S(1)}, u32[]{:S(2)}, u32[]{:S(2)}) collective-permute-start(f32[1,3,128]{1,2,0:T(8,128)S(1)} %get-tuple-element.2090), channel_id=1, source_target_pairs={{0,1},{1,2},{2,3},{3,4},{4,5},{5,6},{6,7},{7,8},{8,9},{9,10},{10,1... | collective-permute-start | bytes 4616 | tf_op jit(solution)/shard_map/ppermute | solution.py:20
  19.8 9.8 %collective-permute-start.3 = (f32[1,3,128]{1,2,0:T(8,128)S(1)}, f32[1,3,128]{1,2,0:T(8,128)S(1)}, u32[]{:S(2)}, u32[]{:S(2)}) collective-permute-start(f32[1,3,128]{1,2,0:T(8,128)S(1)} %get-tuple-element.2089), channel_id=1, source_target_pairs={{1,0},{2,1},{3,2},{4,3},{5,4},{6,5},{7,6},{8,7},{9,8},{10,9},{11,1... | collective-permute-start | bytes 4616 | tf_op jit(solution)/shard_map/ppermute | solution.py:21
  31.3 64.2 %collective-permute-start.6 = (f32[2,3,128]{2,0,1:T(2,128)}, f32[2,3,128]{2,0,1:T(2,128)}, u32[]{:S(2)}, u32[]{:S(2)}) collective-permute-start(f32[2,3,128]{2,0,1:T(2,128)} %pad_maximum_fusion.4), channel_id=1, source_target_pairs={{0,768},{128,896},{1,769},{129,897},{2,770},{130,898},{3,771},{131... | collective-permute-start | bytes 9224 | tf_op jit(solution)/shard_map/ppermute | solution.py:29
  32.6 63.0 %collective-permute-start.7 = (f32[2,3,128]{2,0,1:T(2,128)}, f32[2,3,128]{2,0,1:T(2,128)}, u32[]{:S(2)}, u32[]{:S(2)}) collective-permute-start(f32[2,3,128]{2,0,1:T(2,128)} %pad_maximum_fusion.4), channel_id=1, source_target_pairs={{0,512},{128,640},{256,768},{384,896},{1,513},{129,641},{257,769},... | collective-permute-start | bytes 9224 | tf_op jit(solution)/shard_map/ppermute | solution.py:29
  33.9 61.7 %collective-permute-start.8 = (f32[2,3,128]{2,0,1:T(2,128)}, f32[2,3,128]{2,0,1:T(2,128)}, u32[]{:S(2)}, u32[]{:S(2)}) collective-permute-start(f32[2,3,128]{2,0,1:T(2,128)} %pad_maximum_fusion.4), channel_id=1, source_target_pairs={{0,256},{128,384},{256,512},{384,640},{512,768},{640,896},{1,257},... | collective-permute-start | bytes 9224 | tf_op jit(solution)/shard_map/ppermute | solution.py:29
  83.6 5.6 collective-permute-start.4
  85.8 9.8 %collective-permute-start.5 = (f32[1,3,128]{1,2,0:T(8,128)S(1)}, f32[1,3,128]{1,2,0:T(8,128)S(1)}, u32[]{:S(2)}, u32[]{:S(2)}) collective-permute-start(f32[1,3,128]{1,2,0:T(8,128)S(1)} %get-tuple-element.2087), channel_id=1, source_target_pairs={{1,0},{2,1},{3,2},{4,3},{5,4},{6,5},{7,6},{8,7},{9,8},{10,9},{11,1... | collective-permute-start | bytes 4616 | tf_op jit(solution)/shard_map/ppermute | solution.py:21
  158.5 5.7 collective-permute-start.9
  161.0 9.8 %collective-permute-start.10 = (f32[1,3,128]{1,2,0:T(8,128)S(1)}, f32[1,3,128]{1,2,0:T(8,128)S(1)}, u32[]{:S(2)}, u32[]{:S(2)}) collective-permute-start(f32[1,3,128]{1,2,0:T(8,128)S(1)} %get-tuple-element.2085), channel_id=1, source_target_pairs={{1,0},{2,1},{3,2},{4,3},{5,4},{6,5},{7,6},{8,7},{9,8},{10,9},{11,1... | collective-permute-start | bytes 4616 | tf_op jit(solution)/shard_map/ppermute | solution.py:21
  184.7 60.9 %collective-permute-start.13 = (f32[2,3,128]{2,0,1:T(2,128)}, f32[2,3,128]{2,0,1:T(2,128)}, u32[]{:S(2)}, u32[]{:S(2)}) collective-permute-start(f32[2,3,128]{2,0,1:T(2,128)} %pad_maximum_fusion.5), channel_id=1, source_target_pairs={{0,768},{128,896},{1,769},{129,897},{2,770},{130,898},{3,771},{131... | collective-permute-start | bytes 9224 | tf_op jit(solution)/shard_map/ppermute | solution.py:29
  186.0 59.6 %collective-permute-start.14 = (f32[2,3,128]{2,0,1:T(2,128)}, f32[2,3,128]{2,0,1:T(2,128)}, u32[]{:S(2)}, u32[]{:S(2)}) collective-permute-start(f32[2,3,128]{2,0,1:T(2,128)} %pad_maximum_fusion.5), channel_id=1, source_target_pairs={{0,512},{128,640},{256,768},{384,896},{1,513},{129,641},{257,769},... | collective-permute-start | bytes 9224 | tf_op jit(solution)/shard_map/ppermute | solution.py:29
  187.3 58.3 %collective-permute-start.15 = (f32[2,3,128]{2,0,1:T(2,128)}, f32[2,3,128]{2,0,1:T(2,128)}, u32[]{:S(2)}, u32[]{:S(2)}) collective-permute-start(f32[2,3,128]{2,0,1:T(2,128)} %pad_maximum_fusion.5), channel_id=1, source_target_pairs={{0,256},{128,384},{256,512},{384,640},{512,768},{640,896},{1,257},... | collective-permute-start | bytes 9224 | tf_op jit(solution)/shard_map/ppermute | solution.py:29
  233.8 4.3 collective-permute-start.11
  235.7 9.8 %collective-permute-start.12 = (f32[1,3,128]{1,2,0:T(8,128)S(1)}, f32[1,3,128]{1,2,0:T(8,128)S(1)}, u32[]{:S(2)}, u32[]{:S(2)}) collective-permute-start(f32[1,3,128]{1,2,0:T(8,128)S(1)} %get-tuple-element.2083), channel_id=1, source_target_pairs={{1,0},{2,1},{3,2},{4,3},{5,4},{6,5},{7,6},{8,7},{9,8},{10,9},{11,1... | collective-permute-start | bytes 4616 | tf_op jit(solution)/shard_map/ppermute | solution.py:21
  304.3 6.6 %collective-permute-start.16 = (f32[1,3,128]{1,2,0:T(8,128)S(1)}, f32[1,3,128]{1,2,0:T(8,128)S(1)}, u32[]{:S(2)}, u32[]{:S(2)}) collective-permute-start(f32[1,3,128]{1,2,0:T(8,128)S(1)} %get-tuple-element.2082), channel_id=1, source_target_pairs={{0,1},{1,2},{2,3},{3,4},{4,5},{5,6},{6,7},{7,8},{8,9},{9,10},{10,1... | collective-permute-start | bytes 4616 | tf_op jit(solution)/shard_map/ppermute | solution.py:20
  306.2 9.8 %collective-permute-start.17 = (f32[1,3,128]{1,2,0:T(8,128)S(1)}, f32[1,3,128]{1,2,0:T(8,128)S(1)}, u32[]{:S(2)}, u32[]{:S(2)}) collective-permute-start(f32[1,3,128]{1,2,0:T(8,128)S(1)} %get-tuple-element.2081), channel_id=1, source_target_pairs={{1,0},{2,1},{3,2},{4,3},{5,4},{6,5},{7,6},{8,7},{9,8},{10,9},{11,1... | collective-permute-start | bytes 4616 | tf_op jit(solution)/shard_map/ppermute | solution.py:21
  329.9 61.2 %collective-permute-start.20 = (f32[2,3,128]{2,0,1:T(2,128)}, f32[2,3,128]{2,0,1:T(2,128)}, u32[]{:S(2)}, u32[]{:S(2)}) collective-permute-start(f32[2,3,128]{2,0,1:T(2,128)} %pad_maximum_fusion.6), channel_id=1, source_target_pairs={{0,768},{128,896},{1,769},{129,897},{2,770},{130,898},{3,771},{131... | collective-permute-start | bytes 9224 | tf_op jit(solution)/shard_map/ppermute | solution.py:29
  331.2 59.9 %collective-permute-start.21 = (f32[2,3,128]{2,0,1:T(2,128)}, f32[2,3,128]{2,0,1:T(2,128)}, u32[]{:S(2)}, u32[]{:S(2)}) collective-permute-start(f32[2,3,128]{2,0,1:T(2,128)} %pad_maximum_fusion.6), channel_id=1, source_target_pairs={{0,512},{128,640},{256,768},{384,896},{1,513},{129,641},{257,769},... | collective-permute-start | bytes 9224 | tf_op jit(solution)/shard_map/ppermute | solution.py:29
  332.5 58.6 %collective-permute-start.22 = (f32[2,3,128]{2,0,1:T(2,128)}, f32[2,3,128]{2,0,1:T(2,128)}, u32[]{:S(2)}, u32[]{:S(2)}) collective-permute-start(f32[2,3,128]{2,0,1:T(2,128)} %pad_maximum_fusion.6), channel_id=1, source_target_pairs={{0,256},{128,384},{256,512},{384,640},{512,768},{640,896},{1,257},... | collective-permute-start | bytes 9224 | tf_op jit(solution)/shard_map/ppermute | solution.py:29
  379.0 4.3 collective-permute-start.18
  381.3 9.8 %collective-permute-start.19 = (f32[1,3,128]{1,2,0:T(8,128)S(1)}, f32[1,3,128]{1,2,0:T(8,128)S(1)}, u32[]{:S(2)}, u32[]{:S(2)}) collective-permute-start(f32[1,3,128]{1,2,0:T(8,128)S(1)} %get-tuple-element.2079), channel_id=1, source_target_pairs={{1,0},{2,1},{3,2},{4,3},{5,4},{6,5},{7,6},{8,7},{9,8},{10,9},{11,1... | collective-permute-start | bytes 4616 | tf_op jit(solution)/shard_map/ppermute | solution.py:21
  449.3 6.6 %collective-permute-start.23 = (f32[1,3,128]{1,2,0:T(8,128)S(1)}, f32[1,3,128]{1,2,0:T(8,128)S(1)}, u32[]{:S(2)}, u32[]{:S(2)}) collective-permute-start(f32[1,3,128]{1,2,0:T(8,128)S(1)} %get-tuple-element.2078), channel_id=1, source_target_pairs={{0,1},{1,2},{2,3},{3,4},{4,5},{5,6},{6,7},{7,8},{8,9},{9,10},{10,1... | collective-permute-start | bytes 4616 | tf_op jit(solution)/shard_map/ppermute | solution.py:20
  451.2 9.8 %collective-permute-start.24 = (f32[1,3,128]{1,2,0:T(8,128)S(1)}, f32[1,3,128]{1,2,0:T(8,128)S(1)}, u32[]{:S(2)}, u32[]{:S(2)}) collective-permute-start(f32[1,3,128]{1,2,0:T(8,128)S(1)} %get-tuple-element.2077), channel_id=1, source_target_pairs={{1,0},{2,1},{3,2},{4,3},{5,4},{6,5},{7,6},{8,7},{9,8},{10,9},{11,1... | collective-permute-start | bytes 4616 | tf_op jit(solution)/shard_map/ppermute | solution.py:21
  474.0 53.7 %collective-permute-start.27 = (f32[2,3,128]{2,0,1:T(2,128)}, f32[2,3,128]{2,0,1:T(2,128)S(1)}, u32[]{:S(2)}, u32[]{:S(2)}) collective-permute-start(f32[2,3,128]{2,0,1:T(2,128)} %pad_maximum_fusion.7), channel_id=1, source_target_pairs={{0,768},{128,896},{1,769},{129,897},{2,770},{130,898},{3,771},{131... | collective-permute-start | bytes 9224 | tf_op jit(solution)/shard_map/ppermute | solution.py:29
  475.3 52.4 %collective-permute-start.28 = (f32[2,3,128]{2,0,1:T(2,128)}, f32[2,3,128]{2,0,1:T(2,128)}, u32[]{:S(2)}, u32[]{:S(2)}) collective-permute-start(f32[2,3,128]{2,0,1:T(2,128)} %pad_maximum_fusion.7), channel_id=1, source_target_pairs={{0,512},{128,640},{256,768},{384,896},{1,513},{129,641},{257,769},... | collective-permute-start | bytes 9224 | tf_op jit(solution)/shard_map/ppermute | solution.py:29
  476.6 51.1 %collective-permute-start.29 = (f32[2,3,128]{2,0,1:T(2,128)}, f32[2,3,128]{2,0,1:T(2,128)}, u32[]{:S(2)}, u32[]{:S(2)}) collective-permute-start(f32[2,3,128]{2,0,1:T(2,128)} %pad_maximum_fusion.7), channel_id=1, source_target_pairs={{0,256},{128,384},{256,512},{384,640},{512,768},{640,896},{1,257},... | collective-permute-start | bytes 9224 | tf_op jit(solution)/shard_map/ppermute | solution.py:29
  523.3 5.1 collective-permute-start.25
  525.7 9.8 %collective-permute-start.26 = (f32[1,3,128]{1,2,0:T(8,128)S(1)}, f32[1,3,128]{1,2,0:T(8,128)S(1)}, u32[]{:S(2)}, u32[]{:S(2)}) collective-permute-start(f32[1,3,128]{1,2,0:T(8,128)S(1)} %get-tuple-element.2075), channel_id=1, source_target_pairs={{1,0},{2,1},{3,2},{4,3},{5,4},{6,5},{7,6},{8,7},{9,8},{10,9},{11,1... | collective-permute-start | bytes 4616 | tf_op jit(solution)/shard_map/ppermute | solution.py:21
  600.3 5.0 collective-permute-start.30
  602.2 9.8 %collective-permute-start.31 = (f32[1,3,128]{1,2,0:T(8,128)S(1)}, f32[1,3,128]{1,2,0:T(8,128)S(1)}, u32[]{:S(2)}, u32[]{:S(2)}) collective-permute-start(f32[1,3,128]{1,2,0:T(8,128)S(1)} %get-tuple-element.2073), channel_id=1, source_target_pairs={{1,0},{2,1},{3,2},{4,3},{5,4},{6,5},{7,6},{8,7},{9,8},{10,9},{11,1... | collective-permute-start | bytes 4616 | tf_op jit(solution)/shard_map/ppermute | solution.py:21
  (64 other events, 710.9 us)
where the time goes:
time: 643 us; the launch traced here: 631 us
  other arithmetic  351 us (55%)
  local copies, waits for them, and re-layouts  139 us (22%)
  waiting for transfers between devices  63.8 us (10%)
  starting transfers between devices  62.5 us (10%)
    scatter-add x8, other arithmetic, stiff_force(): jnp.zeros_like(displaced).at[:, flat_nodes]  205 us
    gather x8, local copies, waits for them, and re-layouts, stiff_force(): jnp.take(displaced, flat_nodes, axis=1).reshape(3, node_count, elem_count)  73.9 us
    ppermute x10, waiting for transfers between devices, with_halo(): after = lax.ppermute(leading, axis, down)  63.8 us
    scatter-add x24, other arithmetic, add_layer(): forces.at[:, layer_dst[source]]  48.8 us
    scatter-add x16, other arithmetic, take_slots(): forces.at[:, recv_map[0]].add(from_lower).at[:, recv_map[1]].add(from_upper)  34 us
    select_n x16, other arithmetic, stiff_force(): jnp.take(displaced, flat_nodes, axis=1).reshape(3, node_count, elem_count)  30.3 us
    ppermute x10, starting transfers between devices, with_halo(): before = lax.ppermute(last, axis, up)  25 us
    ppermute x10, starting transfers between devices, with_halo(): after = lax.ppermute(leading, axis, down)  22 us
  transfers between devices with their start and end apart: 32, of which 10 were waited for; matrix products, arithmetic and copies ran while one was open for 31% of the time, Pallas kernels for 0%

commit v1 on v0

v1 whole, which is shorter than its diff:
```python
import functools

import jax
import jax.numpy as jnp
from jax import lax
from jax.experimental import pallas as pl
from jax.experimental.pallas import tpu as pltpu
from jax.sharding import PartitionSpec as P

STEPS = 8
MESH = pl.DeviceIdType.MESH
SHIFT = 13
BIG = 2047 << SHIFT
F32 = jnp.float32
BF16 = jnp.bfloat16


def pad_to(value, unit):
    return -(-value // unit) * unit


class Kind:
    def __init__(self, points, quads, elems, nodes):
        self.P, self.Q, self.E, self.N = points, quads, elems, nodes
        self.LC = elems // 128
        self.NR = nodes // 128
        self.NRP = pad_to(self.NR, 8)
        self.PP = pad_to(points, 8)
        self.QP = pad_to(quads, 8)
        self.KQ = 3 * self.QP
        self.SR = self.LC * self.PP
        self.R = 8
        while self.R < self.SR:
            self.R *= 2
        self.LAST = points * elems // 128
        self.R2 = pad_to(self.LAST + 1, 8)
        self.W = 3 * elems
        self.rows = [k * self.PP + p for k in range(self.LC) for p in range(points)]


def lane_take(x, idx):
    dims = lax.GatherDimensionNumbers(
        offset_dims=(),
        collapsed_slice_dims=(1,),
        start_index_map=(1,),
        operand_batching_dims=(0,),
        start_indices_batching_dims=(0,),
    )
    return lax.gather(
        x, idx[..., None], dims, (1, 1), mode=lax.GatherScatterMode.PROMISE_IN_BOUNDS
    )


def iota2(shape, dim):
    return lax.broadcasted_iota(jnp.int32, shape, dim)


def spread(row):
    return jnp.broadcast_to(row, (8, 128))


def split(x):
    hi = x.astype(BF16).astype(F32)
    return hi, x - hi


def mm(a, b):
    return jnp.dot(a.astype(BF16), b.astype(BF16), preferred_element_type=F32)


def sort_regs(regs):
    count = len(regs)
    depth = count * 8
    row_bits = depth.bit_length() - 1
    sub = iota2((8, 128), 0)
    lane = iota2((8, 128), 1)

    def bit_mask(bit, v):
        if bit < 3:
            return (sub >> bit) & 1
        if bit < row_bits:
            return (v >> (bit - 3)) & 1
        if bit >= row_bits + 7:
            return 0
        return (lane >> (bit - row_bits)) & 1

    total_bits = row_bits + 7
    for m in range(1, total_bits + 1):
        for jb in range(m - 1, -1, -1):
            new = list(regs)
            if 3 <= jb < row_bits:
                step = 1 << (jb - 3)
                for v in range(count):
                    if v & step:
                        continue
                    a, b = regs[v], regs[v + step]
                    low, high = jnp.minimum(a, b), jnp.maximum(a, b)
                    down = bit_mask(m, v)
                    if isinstance(down, int):
                        new[v], new[v + step] = (high, low) if down else (low, high)
                    else:
                        new[v] = jnp.where(down == 1, high, low)
                        new[v + step] = jnp.where(down == 1, low, high)
            else:
                for v in range(count):
                    x = regs[v]
                    if jb < 3:
                        dist = 1 << jb
                        if dist == 4:
                            other = pltpu.roll(x, 4, 0)
                        else:
                            other = jnp.where(
                                bit_mask(jb, v) == 1, pltpu.roll(x, dist, 0), pltpu.roll(x, 8 - dist, 0)
                            )
                    else:
                        dist = 1 << (jb - row_bits)
                        other = lane_take(x, lane ^ dist)
                    take_max = bit_mask(jb, v) ^ bit_mask(m, v)
                    new[v] = jnp.where(take_max == 1, jnp.maximum(x, other), jnp.minimum(x, other))
            regs = new
    return regs


def gather_three(idx_row, idx_lane, load_row, rows):
    out = [jnp.zeros((8, 128), F32) for _ in range(3)]
    for r in rows:
        here = idx_row == r
        for c in range(3):
            out[c] = jnp.where(here, lane_take(spread(load_row(c, r)), idx_lane), out[c])
    return out


def setup_state(kind, disp, vel, u, prev):
    for ref in (u, prev):
        ref[...] = jnp.zeros(ref.shape, F32)
    for c in range(3):
        u[c : c + 1, :] = disp[0, c]
        prev[c : c + 1, :] = disp[0, c] - vel[0, c]


def setup_tables(kind, table, flipped, tpad, d1, d2):
    tpad[...] = jnp.zeros(tpad.shape, F32)
    if flipped:
        tpad[0 : kind.P, 0 : kind.KQ] = table[...]
        across = tpad[...]
        whole = across.T
    else:
        for b in range(3):
            tpad[b * kind.QP : b * kind.QP + kind.Q, 0 : kind.P] = table[b * kind.Q : (b + 1) * kind.Q, :]
        whole = tpad[...]
        across = whole.T
    hi, lo = split(across[0 : kind.PP])
    stack = [hi, hi, lo]
    left = 128 - 3 * kind.PP
    if left:
        stack.append(jnp.zeros((left, 128), F32))
    d1[...] = jnp.concatenate(stack, axis=0).T
    hi, lo = split(-whole[0 : kind.KQ])
    depth = d2.shape[1]
    stack = [hi, hi, lo]
    left = depth - 3 * kind.KQ
    if left:
        stack.append(jnp.zeros((left, 128), F32))
    stack = jnp.concatenate(stack, axis=0)
    for k in range(depth // 128):
        d2[:, k * 128 : (k + 1) * 128] = stack[k * 128 : (k + 1) * 128].T


def setup_plan(kind, nodes, node_s, key_s, plan_s, pos_s):
    sub = iota2((8, 128), 0)
    lane = iota2((8, 128), 1)
    node_s[...] = jnp.zeros(node_s.shape, jnp.int32)
    for k in range(kind.LC):
        for p in range(kind.P):
            at = k * kind.PP + p
            node_s[at : at + 1, :] = nodes[0, p, :, k * 128 : (k + 1) * 128]
    regs = []
    for v in range(kind.R // 8):
        if v * 8 >= kind.SR:
            regs.append(jnp.full((8, 128), BIG, jnp.int32))
            continue
        row = sub + v * 8
        inside = (row % kind.PP) < kind.P
        found = jnp.where(inside, node_s[v * 8 : v * 8 + 8, :], BIG >> SHIFT)
        regs.append((found << SHIFT) | (row << 7) | lane)
    regs = sort_regs(regs)
    for v, reg in enumerate(regs):
        key_s[v * 8 : v * 8 + 8, :] = reg
    bits = kind.R.bit_length() - 1
    for v in range(kind.R2 // 8):
        place = (sub + v * 8) * 128 + lane
        src_row, src_lane = place & (kind.R - 1), place >> bits
        out = jnp.zeros((8, 128), jnp.int32)
        for r in range(kind.R):
            out = jnp.where(src_row == r, lane_take(spread(key_s[r : r + 1, :]), src_lane), out)
        live = out < BIG
        slot = out & ((1 << SHIFT) - 1)
        plan_s[0, v * 8 : v * 8 + 8, :] = jnp.where(live, slot >> 7, 1000)
        plan_s[1, v * 8 : v * 8 + 8, :] = slot & 127
    last = spread(key_s[kind.R - 1 : kind.R, :])
    for v in range(kind.NRP // 8):
        target = ((sub + v * 8) * 128 + lane + 1) << SHIFT
        column = jnp.zeros((8, 128), jnp.int32)
        for step in (64, 32, 16, 8, 4, 2, 1):
            column = jnp.where(lane_take(last, column + (step - 1)) < target, column + step, column)
        count = jnp.zeros((8, 128), jnp.int32)
        for r in range(kind.R):
            count = count + jnp.where(lane_take(spread(key_s[r : r + 1, :]), column) < target, 1, 0)
        place = column * kind.R + count
        pos_s[0, v * 8 : v * 8 + 8, :] = place >> 7
        pos_s[1, v * 8 : v * 8 + 8, :] = place & 127


def setup_scan(scan):
    row = iota2(scan.shape, 0) % 128
    col = iota2(scan.shape, 1)
    scan[...] = jnp.where(row < col, 1.0, 0.0).astype(BF16)


def rows_ahead(kind, totals):
    sub = iota2((8, 128), 0)
    run = jnp.zeros((8, 128), F32)
    out = []
    for v in range(kind.R2 // 8):
        upto = totals[v * 8 : v * 8 + 8]
        for dist in (1, 2, 4):
            upto = upto + jnp.where(sub >= dist, pltpu.roll(upto, dist, 0), 0.0)
        out.append(run + jnp.where(sub >= 1, pltpu.roll(upto, 1, 0), 0.0))
        run = run + jnp.broadcast_to(upto[7:8], (8, 128))
    return out


def setup_hot(kind, maps, hot):
    rows = iota2((kind.N, 128), 0)
    for k, load in enumerate(maps):
        hot[:, k * 128 : (k + 1) * 128] = jnp.where(rows == load(), 1.0, 0.0).astype(BF16)


def stiff_force(kind, u, coef, node_s, plan_s, pos_s, d1, d2, scan, fe_s, cx_s, f_s):
    blocks = {}
    for k in range(kind.LC):
        for v in range(kind.PP // 8):
            at = k * kind.PP + v * 8
            index = node_s[at : at + 8, :]
            found = gather_three(
                index >> 7,
                index & 127,
                lambda c, r: u[c : c + 1, r * 128 : (r + 1) * 128],
                range(kind.NR),
            )
            for c in range(3):
                blocks[c, k, v] = found[c]
    chunks = [(c, k) for c in range(3) for k in range(kind.LC)]
    cols = []
    for c, k in chunks:
        ve = jnp.concatenate([blocks[c, k, v] for v in range(kind.PP // 8)], axis=0)
        hi, lo = split(ve)
        parts = [hi, lo, hi]
        left = 128 - 3 * kind.PP
        if left:
            parts.append(jnp.zeros((left, 128), F32))
        cols.append(jnp.concatenate(parts, axis=0).astype(BF16))
    gathered = jnp.concatenate(cols, axis=1)
    grad = jnp.dot(d1[0 : kind.KQ, :].astype(BF16), gathered, preferred_element_type=F32)
    cols = []
    depth = d2.shape[1]
    for i, (c, k) in enumerate(chunks):
        piece = grad[:, i * 128 : (i + 1) * 128]
        terms = []
        for a in range(3):
            total = coef(a, 0, k) * piece[0 : kind.QP]
            for b in (1, 2):
                total = total + coef(a, b, k) * piece[b * kind.QP : (b + 1) * kind.QP]
            terms.append(total)
        flux = jnp.concatenate(terms, axis=0)
        hi, lo = split(flux)
        parts = [hi, lo, hi]
        left = depth - 3 * kind.KQ
        if left:
            parts.append(jnp.zeros((left, 128), F32))
        cols.append(jnp.concatenate(parts, axis=0).astype(BF16))
    flux = jnp.concatenate(cols, axis=1)
    fe = jnp.dot(d2[0 : kind.PP, :].astype(BF16), flux, preferred_element_type=F32)
    for i, (c, k) in enumerate(chunks):
        fe_s[c, k * kind.PP : (k + 1) * kind.PP, :] = fe[:, i * 128 : (i + 1) * 128]
    cols = [[], [], []]
    for v in range(kind.R2 // 8):
        found = gather_three(
            plan_s[0, v * 8 : v * 8 + 8, :],
            plan_s[1, v * 8 : v * 8 + 8, :],
            lambda c, r: fe_s[c, r : r + 1, :],
            kind.rows,
        )
        for c in range(3):
            cols[c].append(found[c])
    both = []
    for c in range(3):
        hi, lo = split(jnp.concatenate(cols[c], axis=0))
        both.append(jnp.concatenate([hi, lo], axis=1).astype(BF16))
    sums = jnp.dot(jnp.concatenate(both, axis=0), scan[...], preferred_element_type=F32)
    for c in range(3):
        rows = sums[c * kind.R2 : (c + 1) * kind.R2]
        for v, ahead in enumerate(rows_ahead(kind, rows[:, 128:256])):
            cx_s[c, v * 8 : v * 8 + 8, :] = rows[v * 8 : v * 8 + 8, 0:128] + ahead
    corner_row = iota2((kind.NRP, 128), 0)
    corner_lane = iota2((kind.NRP, 128), 1)
    found = [
        gather_three(
            pos_s[0, v * 8 : v * 8 + 8, :],
            pos_s[1, v * 8 : v * 8 + 8, :],
            lambda c, r: cx_s[c, r : r + 1, :],
            range(kind.LAST + 1),
        )
        for v in range(kind.NRP // 8)
    ]
    for c in range(3):
        ends = jnp.concatenate([block[c] for block in found], axis=0)
        before = pltpu.roll(ends, 1, 1)
        above = pltpu.roll(before, 1, 0)
        before = jnp.where(corner_lane == 0, above, before)
        before = jnp.where((corner_lane == 0) & (corner_row == 0), 0.0, before)
        forces = ends - before
        for r in range(kind.NR):
            f_s[c : c + 1, r * 128 : (r + 1) * 128] = forces[r : r + 1, :]


def pick(kind, source, index):
    idx_row, idx_lane = spread(index >> 7), spread(index & 127)
    out = jnp.zeros((8, 128), F32)
    for r in range(kind.NR):
        out = jnp.where(
            idx_row == r, lane_take(source[:, r * 128 : (r + 1) * 128], idx_lane), out
        )
    return out


def drop(kind, parts, hot):
    r = jnp.concatenate(parts, axis=1)
    hi, lo = split(r)
    both = jnp.concatenate([hi, lo], axis=0).astype(BF16)
    out = lax.dot_general(
        both, hot[...], (((1,), (1,)), ((), ())), preferred_element_type=F32
    )
    return out[0:8] + out[8:16]


def body(
    reg, site, reg_groups, site_groups, sub_count,
    reg_disp, reg_vel, site_disp, site_vel, reg_nodes, site_nodes, reg_coefs, site_coefs,
    reg_table, site_table, reg_minv, site_minv, reg_send, reg_recv, site_send, site_recv,
    slot_fill, layer_src, layer_fill, layer_dst, layer_stiff,
    reg_out, site_out,
    u_r, prev_r, f_r, tpad_r, d1_r, d2_r, node_r, key_r, plan_r, pos_r, hot_r, fe_r, cx_r, coef_r,
    u_s, prev_s, f_s, tpad_s, d1_s, d2_s, node_s, key_s, plan_s, pos_s, hot_s, fe_s, cx_s,
    hot_l, scan, sends, recvs, layer_out, layer_in,
    send_sem, recv_sem, layer_send_sem, layer_recv_sem,
):
    grp = lax.axis_index("grp")
    sub = lax.axis_index("sub")
    is_site = grp >= reg_groups
    has_lower = sub > 0
    has_upper = sub < sub_count - 1
    source = grp // site_groups
    target = reg_groups + grp % site_groups
    barrier = pltpu.get_barrier_semaphore()

    def hello(g, s):
        pl.semaphore_signal(barrier, inc=1, device_id=(g, s), device_id_type=MESH)

    @pl.when(has_lower)
    def _():
        hello(grp, sub - 1)

    @pl.when(has_upper)
    def _():
        hello(grp, sub + 1)

    @pl.when(is_site)
    def _():
        for m in range(3):
            hello(m * site_groups + grp - reg_groups, sub)

    @pl.when(jnp.logical_not(is_site))
    def _():
        hello(target, sub)

    for there, side in ((has_lower, 0), (has_upper, 1)):

        @pl.when(jnp.logical_not(there))
        def _():
            for n in range(STEPS):
                recvs[n, side] = jnp.zeros((8, 128), F32)

    lane = iota2((8, 128), 1)
    greeted = has_lower.astype(jnp.int32) + has_upper.astype(jnp.int32) + jnp.where(is_site, 3, 1)

    def edge(n, side):
        peer = sub - 1 if side == 0 else sub + 1
        return pltpu.make_async_remote_copy(
            src_ref=sends.at[n, side],
            dst_ref=recvs.at[n, 1 - side],
            send_sem=send_sem.at[n, side],
            recv_sem=recv_sem.at[n, 1 - side],
            device_id=(grp, peer),
            device_id_type=MESH,
        )

    def layer_copy(n, m):
        return pltpu.make_async_remote_copy(
            src_ref=layer_out.at[n],
            dst_ref=layer_in.at[n, m],
            send_sem=layer_send_sem.at[n],
            recv_sem=layer_recv_sem.at[n, m],
            device_id=(target, sub),
            device_id_type=MESH,
        )

    sides = ((has_lower, 0), (has_upper, 1))

    def exchange(kind, n, f, send_map, fills):
        for there, side in sides:
            found = pick(kind, f, send_map[0, 0, side : side + 1, :])
            sends[n, side] = jnp.where(lane < fills[side], found, 0.0)

            @pl.when(there)
            def _():
                edge(n, side).start()

    def arrive(n):
        for there, side in sides:

            @pl.when(there)
            def _():
                edge(n, 1 - side).wait_recv()

    def finish(n, carry):
        for there, side in sides:

            @pl.when(there)
            def _():
                edge(n, side).wait_send()

        return carry

    setup_scan(scan)

    @pl.when(jnp.logical_not(is_site))
    def _():
        kind = reg
        setup_state(kind, reg_disp, reg_vel, u_r, prev_r)
        f_r[...] = jnp.zeros(f_r.shape, F32)
        setup_tables(kind, reg_table, False, tpad_r, d1_r, d2_r)
        coef_r[...] = jnp.zeros(coef_r.shape, F32)
        coef_r[:, :, 0 : kind.Q, :] = reg_coefs[0, 0]
        setup_plan(kind, reg_nodes, node_r, key_r, plan_r, pos_r)
        setup_hot(kind, [lambda i=i: reg_recv[0, 0, i : i + 1, :] for i in range(2)], hot_r)
        pl.semaphore_wait(barrier, greeted)
        fills = (slot_fill[0, 0, 0], slot_fill[0, 0, 1])

        def step(n, carry):
            stiff_force(
                kind, u_r, lambda a, b, k: coef_r[a, b, :, k * 128 : (k + 1) * 128],
                node_r, plan_r, pos_r, d1_r, d2_r, scan, fe_r, cx_r, f_r,
            )
            exchange(kind, n, f_r, reg_send, fills)
            minv = reg_minv[0]
            now = u_r[...]
            ahead = 2.0 * now - prev_r[...] + minv * f_r[...]
            prev_r[...] = now
            arrive(n)
            u_r[...] = ahead + minv * drop(kind, [recvs[n, 0], recvs[n, 1]], hot_r)
            found = pick(kind, u_r, layer_src[0])
            layer_out[n] = jnp.where(lane < layer_fill[0, 0], found, 0.0)
            layer_copy(n, source).start()
            return carry

        lax.fori_loop(0, STEPS, step, 0)
        for c in range(3):
            reg_out[0, c] = u_r[c : c + 1, :]
        site_out[...] = jnp.zeros(site_out.shape, F32)

        def drain(n, carry):
            layer_copy(n, source).wait_send()
            return finish(n, carry)

        lax.fori_loop(0, STEPS, drain, 0)

    @pl.when(is_site)
    def _():
        kind = site
        setup_state(kind, site_disp, site_vel, u_s, prev_s)
        f_s[...] = jnp.zeros(f_s.shape, F32)
        setup_tables(kind, site_table, True, tpad_s, d1_s, d2_s)
        setup_plan(kind, site_nodes, node_s, key_s, plan_s, pos_s)
        setup_hot(kind, [lambda i=i: site_recv[0, 0, i : i + 1, :] for i in range(2)], hot_s)
        setup_hot(kind, [lambda i=i: layer_dst[0, i] for i in range(3)], hot_l)
        pl.semaphore_wait(barrier, greeted)
        fills = (slot_fill[0, 0, 2], slot_fill[0, 0, 3])

        def step(n, carry):
            stiff_force(
                kind, u_s, lambda a, b, k: site_coefs[0, 0, a, b],
                node_s, plan_s, pos_s, d1_s, d2_s, scan, fe_s, cx_s, f_s,
            )
            exchange(kind, n, f_s, site_send, fills)
            minv = site_minv[0]
            now = u_s[...]
            ahead = 2.0 * now - prev_s[...] + minv * f_s[...]
            prev_s[...] = now
            parts = []
            for m in range(3):
                layer_copy(n, m).wait_recv()
                parts.append(layer_in[n, m] * layer_stiff[0, m])
            ahead = ahead + minv * drop(kind, parts, hot_l)
            arrive(n)
            u_s[...] = ahead + minv * drop(kind, [recvs[n, 0], recvs[n, 1]], hot_s)
            return carry

        lax.fori_loop(0, STEPS, step, 0)
        for c in range(3):
            site_out[0, c] = u_s[c : c + 1, :]
        reg_out[...] = jnp.zeros(reg_out.shape, F32)
        lax.fori_loop(0, STEPS, finish, 0)


def kind_scratch(kind):
    depth = pad_to(3 * kind.KQ, 128)
    i32 = jnp.int32
    return [
        pltpu.VMEM((8, kind.N), F32),
        pltpu.VMEM((8, kind.N), F32),
        pltpu.VMEM((8, kind.N), F32),
        pltpu.VMEM((128, 128), F32),
        pltpu.VMEM((128, 128), F32),
        pltpu.VMEM((128, depth), F32),
        pltpu.VMEM((kind.SR, 128), i32),
        pltpu.VMEM((kind.R, 128), i32),
        pltpu.VMEM((2, kind.R2, 128), i32),
        pltpu.VMEM((2, kind.NRP, 128), i32),
        pltpu.VMEM((kind.N, 256), BF16),
        pltpu.VMEM((3, kind.SR, 128), F32),
        pltpu.VMEM((3, kind.R2, 128), F32),
    ]


def shards(*args):
    group_count = lax.axis_size("grp")
    site_groups = group_count // 4
    reg_groups = 3 * site_groups
    reg = Kind(args[4].shape[2], args[6].shape[4], args[4].shape[3], args[0].shape[3])
    site = Kind(args[5].shape[2], args[7].shape[4], args[5].shape[3], args[2].shape[3])
    args = list(args)
    for i in (0, 1, 2, 3, 4, 5, 19, 20):
        args[i] = jnp.transpose(args[i], (0, 2, 1, 3))
    args[9] = args[9].T
    vmem = pl.BlockSpec(memory_space=pltpu.VMEM)
    smem = pl.BlockSpec(memory_space=pltpu.SMEM)
    in_specs = [vmem] * len(args)
    in_specs[16] = smem
    in_specs[18] = smem
    kernel = functools.partial(body, reg, site, reg_groups, site_groups, lax.axis_size("sub"))
    outs = pl.pallas_call(
        kernel,
        name="drm_window",
        out_shape=(
            jax.ShapeDtypeStruct((1, 3, 1, reg.N), F32),
            jax.ShapeDtypeStruct((1, 3, 1, site.N), F32),
        ),
        in_specs=in_specs,
        out_specs=(vmem, vmem),
        scratch_shapes=kind_scratch(reg)
        + [pltpu.VMEM((3, 3, reg.QP, reg.E), F32)]
        + kind_scratch(site)
        + [
            pltpu.VMEM((site.N, 384), BF16),
            pltpu.VMEM((256, 256), BF16),
            pltpu.VMEM((STEPS, 2, 8, 128), F32),
            pltpu.VMEM((STEPS, 2, 8, 128), F32),
            pltpu.VMEM((STEPS, 8, 128), F32),
            pltpu.VMEM((STEPS, 3, 8, 128), F32),
            pltpu.SemaphoreType.DMA((STEPS, 2)),
            pltpu.SemaphoreType.DMA((STEPS, 2)),
            pltpu.SemaphoreType.DMA((STEPS,)),
            pltpu.SemaphoreType.DMA((STEPS, 3)),
        ],
        compiler_params=pltpu.CompilerParams(collective_id=0, has_side_effects=True),
    )(*args)
    return tuple(jnp.transpose(out, (0, 2, 1, 3)) for out in outs)


def solution(mesh):
    whole = P("grp", "sub")
    specs = [whole] * 21
    specs[8] = P()
    specs[9] = P()
    return jax.shard_map(
        shards,
        mesh=mesh,
        in_specs=tuple(specs),
        out_specs=(whole, whole),
        check_vma=False,
    )
```

time: 643 us -> 66.1 us (0.10)
  the two profiles are of different devices: /device:TPU:255 before, /device:TPU:511 now
where the time goes in v1:
time: 66.1 us; the launch traced here: 65.8 us
  Pallas kernels  61.9 us (94%)
  local copies, waits for them, and re-layouts  2.6 us (4%)
  between operations  1.3 us (2%)
    pallas_call x1, Pallas kernels, shards(): pl.pallas_call(kernel, name='drm_window', out_shape=(jax.ShapeDtypeStruct...  61.9 us
    unnamed x4, local copies, waits for them, and re-layouts  2.6 us

profile of v1, /device:TPU:511, one launch (start us, length us, event | category | flops | bytes accessed | tf_op | source)
XLA Modules:
  0.0 65.8 jit_solution(7640935704850453816)
XLA Ops:
  1.3 61.9 %drm_window.1 = (f32[1,3,1,384]{3,2,1,0:T(1,128)}, f32[1,3,1,1536]{3,2,1,0:T(1,128)}) custom-call(f32[1,3,1,384]{3,2,1,0:T(1,128)} %bitcast.22, f32[1,3,1,384]{3,2,1,0:T(1,128)} %bitcast.23, f32[1,3,1,1536]{3,2,1,0:T(1,128)} %bitcast.16, f32[1,3,1,1536]{3,2,1,0:T(1,128)} %bitcast.17, s32[1,10,1,256]{3,2,1,0:T(1,128)} %bitcast.20, ...), custom_call_target="tpu_custom_call" | custom-call | tf_op jit(solution)/shard_map/drm_window/pallas_call | solution.py:562
  63.2 0.0 copy-start
  63.2 0.7 %copy-done = f32[1,3,1,384]{3,2,1,0:T(1,128)S(1)} copy-done((f32[1,3,1,384]{3,2,1,0:T(1,128)S(1)}, f32[1,3,1,384]{3,2,1,0:T(1,128)}, u32[]{:S(2)}) %copy-start) | copy-done | bytes 4632
  63.9 0.6 copy.28
  64.5 1.3 %copy.29 = f32[1,1,3,1536]{3,1,2,0:T(1,128)} copy(f32[1,1,3,1536]{3,1,2,0:T(1,128)} %bitcast.18) | data formatting | bytes 36864
Async XLA Ops:
  63.2 0.7 %copy-start = (f32[1,3,1,384]{3,2,1,0:T(1,128)S(1)}, f32[1,3,1,384]{3,2,1,0:T(1,128)}, u32[]{:S(2)}) copy-start(f32[1,3,1,384]{3,2,1,0:T(1,128)} %get-tuple-element.4) | copy-start | bytes 13828

commit v2 on v1

--- a/solution.py
+++ b/solution.py
@@ -29,13 +29,7 @@
         self.QP = pad_to(quads, 8)
         self.KQ = 3 * self.QP
         self.SR = self.LC * self.PP
-        self.R = 8
-        while self.R < self.SR:
-            self.R *= 2
-        self.LAST = points * elems // 128
-        self.R2 = pad_to(self.LAST + 1, 8)
-        self.W = 3 * elems
-        self.rows = [k * self.PP + p for k in range(self.LC) for p in range(points)]
+        self.W8 = self.SR // 8
 
 
 def lane_take(x, idx):
@@ -166,7 +160,7 @@
         d2[:, k * 128 : (k + 1) * 128] = stack[k * 128 : (k + 1) * 128].T
 
 
-def setup_plan(kind, nodes, node_s, key_s, plan_s, pos_s):
+def setup_plan(kind, nodes, send_map, node_s, key_s, plan_s, pos_s):
     sub = iota2((8, 128), 0)
     lane = iota2((8, 128), 1)
     node_s[...] = jnp.zeros(node_s.shape, jnp.int32)
@@ -174,41 +168,33 @@
         for p in range(kind.P):
             at = k * kind.PP + p
             node_s[at : at + 1, :] = nodes[0, p, :, k * 128 : (k + 1) * 128]
-    regs = []
-    for v in range(kind.R // 8):
-        if v * 8 >= kind.SR:
-            regs.append(jnp.full((8, 128), BIG, jnp.int32))
-            continue
-        row = sub + v * 8
-        inside = (row % kind.PP) < kind.P
-        found = jnp.where(inside, node_s[v * 8 : v * 8 + 8, :], BIG >> SHIFT)
-        regs.append((found << SHIFT) | (row << 7) | lane)
-    regs = sort_regs(regs)
-    for v, reg in enumerate(regs):
-        key_s[v * 8 : v * 8 + 8, :] = reg
-    bits = kind.R.bit_length() - 1
-    for v in range(kind.R2 // 8):
-        place = (sub + v * 8) * 128 + lane
-        src_row, src_lane = place & (kind.R - 1), place >> bits
-        out = jnp.zeros((8, 128), jnp.int32)
-        for r in range(kind.R):
-            out = jnp.where(src_row == r, lane_take(spread(key_s[r : r + 1, :]), src_lane), out)
-        live = out < BIG
-        slot = out & ((1 << SHIFT) - 1)
-        plan_s[0, v * 8 : v * 8 + 8, :] = jnp.where(live, slot >> 7, 1000)
-        plan_s[1, v * 8 : v * 8 + 8, :] = slot & 127
-    last = spread(key_s[kind.R - 1 : kind.R, :])
-    for v in range(kind.NRP // 8):
-        target = ((sub + v * 8) * 128 + lane + 1) << SHIFT
-        column = jnp.zeros((8, 128), jnp.int32)
-        for step in (64, 32, 16, 8, 4, 2, 1):
-            column = jnp.where(lane_take(last, column + (step - 1)) < target, column + step, column)
-        count = jnp.zeros((8, 128), jnp.int32)
-        for r in range(kind.R):
-            count = count + jnp.where(lane_take(spread(key_s[r : r + 1, :]), column) < target, 1, 0)
-        place = column * kind.R + count
-        pos_s[0, v * 8 : v * 8 + 8, :] = place >> 7
-        pos_s[1, v * 8 : v * 8 + 8, :] = place & 127
+    for w in range(kind.W8):
+        inside = ((sub + w * 8) % kind.PP) < kind.P
+        found = jnp.where(inside, node_s[w * 8 : w * 8 + 8, :], BIG >> SHIFT)
+        keys = sort_regs([(found << SHIFT) | (sub << 7) | lane])[0]
+        key_s[w * 8 : w * 8 + 8, :] = keys
+        slot = keys & ((1 << SHIFT) - 1)
+        plan_s[0, w * 8 : w * 8 + 8, :] = jnp.where(keys < BIG, slot >> 7, 1000)
+        plan_s[1, w * 8 : w * 8 + 8, :] = slot & 127
+    targets = [((sub + v * 8) * 128 + lane + 1) << SHIFT for v in range(kind.NRP // 8)]
+    sent = jnp.zeros((8, 128), jnp.int32)
+    for side in range(2):
+        wanted = spread(send_map[0, 0, side : side + 1, :])
+        sent = jnp.where(sub == 2 * side, wanted + 1, sent)
+        sent = jnp.where(sub == 2 * side + 1, wanted, sent)
+    targets.append(sent << SHIFT)
+    for w in range(kind.W8):
+        last = spread(key_s[w * 8 + 7 : w * 8 + 8, :])
+        for v, target in enumerate(targets):
+            column = jnp.zeros((8, 128), jnp.int32)
+            for step in (64, 32, 16, 8, 4, 2, 1):
+                column = jnp.where(lane_take(last, column + (step - 1)) < target, column + step, column)
+            place = column * 8 - 1
+            for r in range(8):
+                row = spread(key_s[w * 8 + r : w * 8 + r + 1, :])
+                place = place + jnp.where(lane_take(row, column) < target, 1, 0)
+            pos_s[v, w, 0] = jnp.where(place < 0, 1000, place & 7)
+            pos_s[v, w, 1] = jnp.where(place < 0, 0, place >> 3)
 
 
 def setup_scan(scan):
@@ -217,26 +203,13 @@
     scan[...] = jnp.where(row < col, 1.0, 0.0).astype(BF16)
 
 
-def rows_ahead(kind, totals):
-    sub = iota2((8, 128), 0)
-    run = jnp.zeros((8, 128), F32)
-    out = []
-    for v in range(kind.R2 // 8):
-        upto = totals[v * 8 : v * 8 + 8]
-        for dist in (1, 2, 4):
-            upto = upto + jnp.where(sub >= dist, pltpu.roll(upto, dist, 0), 0.0)
-        out.append(run + jnp.where(sub >= 1, pltpu.roll(upto, 1, 0), 0.0))
-        run = run + jnp.broadcast_to(upto[7:8], (8, 128))
-    return out
-
-
 def setup_hot(kind, maps, hot):
     rows = iota2((kind.N, 128), 0)
     for k, load in enumerate(maps):
         hot[:, k * 128 : (k + 1) * 128] = jnp.where(rows == load(), 1.0, 0.0).astype(BF16)
 
 
-def stiff_force(kind, u, coef, node_s, plan_s, pos_s, d1, d2, scan, fe_s, cx_s, f_s):
+def stiff_force(kind, u, coef, node_s, plan_s, d1, d2, scan, fe_s, cx_s):
     blocks = {}
     for k in range(kind.LC):
         for v in range(kind.PP // 8):
@@ -283,36 +256,52 @@
     fe = jnp.dot(d2[0 : kind.PP, :].astype(BF16), flux, preferred_element_type=F32)
     for i, (c, k) in enumerate(chunks):
         fe_s[c, k * kind.PP : (k + 1) * kind.PP, :] = fe[:, i * 128 : (i + 1) * 128]
-    cols = [[], [], []]
-    for v in range(kind.R2 // 8):
+    sub = iota2((8, 128), 0)
+    terms = {}
+    both = []
+    for w in range(kind.W8):
         found = gather_three(
-            plan_s[0, v * 8 : v * 8 + 8, :],
-            plan_s[1, v * 8 : v * 8 + 8, :],
-            lambda c, r: fe_s[c, r : r + 1, :],
-            kind.rows,
+            plan_s[0, w * 8 : w * 8 + 8, :],
+            plan_s[1, w * 8 : w * 8 + 8, :],
+            lambda c, r: fe_s[c, w * 8 + r : w * 8 + r + 1, :],
+            [r for r in range(8) if (w * 8 + r) % kind.PP < kind.P],
         )
         for c in range(3):
-            cols[c].append(found[c])
-    both = []
-    for c in range(3):
-        hi, lo = split(jnp.concatenate(cols[c], axis=0))
-        both.append(jnp.concatenate([hi, lo], axis=1).astype(BF16))
-    sums = jnp.dot(jnp.concatenate(both, axis=0), scan[...], preferred_element_type=F32)
-    for c in range(3):
-        rows = sums[c * kind.R2 : (c + 1) * kind.R2]
-        for v, ahead in enumerate(rows_ahead(kind, rows[:, 128:256])):
-            cx_s[c, v * 8 : v * 8 + 8, :] = rows[v * 8 : v * 8 + 8, 0:128] + ahead
+            hi, lo = split(found[c])
+            both.append(jnp.concatenate([hi, lo], axis=1))
+            upto = found[c]
+            for dist in (1, 2, 4):
+                upto = upto + jnp.where(sub >= dist, pltpu.roll(upto, dist, 0), 0.0)
+            terms[w, c] = upto
+    sums = jnp.dot(
+        jnp.concatenate(both, axis=0).astype(BF16), scan[...], preferred_element_type=F32
+    )
+    for w in range(kind.W8):
+        for c in range(3):
+            at = (w * 3 + c) * 8
+            ahead = sums[at : at + 8]
+            for dist in (4, 2, 1):
+                ahead = ahead + pltpu.roll(ahead, dist, 0)
+            cx_s[c, w * 8 : w * 8 + 8, :] = terms[w, c] + ahead
+
+
+def read_ends(kind, v, pos_s, cx_s):
+    total = None
+    for w in range(kind.W8):
+        found = gather_three(
+            pos_s[v, w, 0],
+            pos_s[v, w, 1],
+            lambda c, r: cx_s[c, w * 8 + r : w * 8 + r + 1, :],
+            range(8),
+        )
+        total = found if total is None else [a + b for a, b in zip(total, found)]
+    return total
+
+
+def node_forces(kind, pos_s, cx_s, f_s):
     corner_row = iota2((kind.NRP, 128), 0)
     corner_lane = iota2((kind.NRP, 128), 1)
-    found = [
-        gather_three(
-            pos_s[0, v * 8 : v * 8 + 8, :],
-            pos_s[1, v * 8 : v * 8 + 8, :],
-            lambda c, r: cx_s[c, r : r + 1, :],
-            range(kind.LAST + 1),
-        )
-        for v in range(kind.NRP // 8)
-    ]
+    found = [read_ends(kind, v, pos_s, cx_s) for v in range(kind.NRP // 8)]
     for c in range(3):
         ends = jnp.concatenate([block[c] for block in found], axis=0)
         before = pltpu.roll(ends, 1, 1)
@@ -417,10 +406,12 @@
 
     sides = ((has_lower, 0), (has_upper, 1))
 
-    def exchange(kind, n, f, send_map, fills):
+    def exchange(kind, n, pos, cx, fills):
+        found = read_ends(kind, kind.NRP // 8, pos, cx)
         for there, side in sides:
-            found = pick(kind, f, send_map[0, 0, side : side + 1, :])
-            sends[n, side] = jnp.where(lane < fills[side], found, 0.0)
+            for c in range(3):
+                force = found[c][2 * side : 2 * side + 1] - found[c][2 * side + 1 : 2 * side + 2]
+                sends[n, side, c : c + 1, :] = jnp.where(lane[0:1] < fills[side], force, 0.0)
 
             @pl.when(there)
             def _():
@@ -443,6 +434,7 @@
         return carry
 
     setup_scan(scan)
+    sends[...] = jnp.zeros(sends.shape, F32)
 
     @pl.when(jnp.logical_not(is_site))
     def _():
@@ -452,7 +444,7 @@
         setup_tables(kind, reg_table, False, tpad_r, d1_r, d2_r)
         coef_r[...] = jnp.zeros(coef_r.shape, F32)
         coef_r[:, :, 0 : kind.Q, :] = reg_coefs[0, 0]
-        setup_plan(kind, reg_nodes, node_r, key_r, plan_r, pos_r)
+        setup_plan(kind, reg_nodes, reg_send, node_r, key_r, plan_r, pos_r)
         setup_hot(kind, [lambda i=i: reg_recv[0, 0, i : i + 1, :] for i in range(2)], hot_r)
         pl.semaphore_wait(barrier, greeted)
         fills = (slot_fill[0, 0, 0], slot_fill[0, 0, 1])
@@ -460,9 +452,10 @@
         def step(n, carry):
             stiff_force(
                 kind, u_r, lambda a, b, k: coef_r[a, b, :, k * 128 : (k + 1) * 128],
-                node_r, plan_r, pos_r, d1_r, d2_r, scan, fe_r, cx_r, f_r,
+                node_r, plan_r, d1_r, d2_r, scan, fe_r, cx_r,
             )
-            exchange(kind, n, f_r, reg_send, fills)
+            exchange(kind, n, pos_r, cx_r, fills)
+            node_forces(kind, pos_r, cx_r, f_r)
             minv = reg_minv[0]
             now = u_r[...]
             ahead = 2.0 * now - prev_r[...] + minv * f_r[...]
@@ -491,7 +484,7 @@
         setup_state(kind, site_disp, site_vel, u_s, prev_s)
         f_s[...] = jnp.zeros(f_s.shape, F32)
         setup_tables(kind, site_table, True, tpad_s, d1_s, d2_s)
-        setup_plan(kind, site_nodes, node_s, key_s, plan_s, pos_s)
+        setup_plan(kind, site_nodes, site_send, node_s, key_s, plan_s, pos_s)
         setup_hot(kind, [lambda i=i: site_recv[0, 0, i : i + 1, :] for i in range(2)], hot_s)
         setup_hot(kind, [lambda i=i: layer_dst[0, i] for i in range(3)], hot_l)
         pl.semaphore_wait(barrier, greeted)
@@ -500,9 +493,10 @@
         def step(n, carry):
             stiff_force(
                 kind, u_s, lambda a, b, k: site_coefs[0, 0, a, b],
-                node_s, plan_s, pos_s, d1_s, d2_s, scan, fe_s, cx_s, f_s,
+                node_s, plan_s, d1_s, d2_s, scan, fe_s, cx_s,
             )
-            exchange(kind, n, f_s, site_send, fills)
+            exchange(kind, n, pos_s, cx_s, fills)
+            node_forces(kind, pos_s, cx_s, f_s)
             minv = site_minv[0]
             now = u_s[...]
             ahead = 2.0 * now - prev_s[...] + minv * f_s[...]
@@ -534,12 +528,12 @@
         pltpu.VMEM((128, 128), F32),
         pltpu.VMEM((128, depth), F32),
         pltpu.VMEM((kind.SR, 128), i32),
-        pltpu.VMEM((kind.R, 128), i32),
-        pltpu.VMEM((2, kind.R2, 128), i32),
-        pltpu.VMEM((2, kind.NRP, 128), i32),
+        pltpu.VMEM((kind.SR, 128), i32),
+        pltpu.VMEM((2, kind.SR, 128), i32),
+        pltpu.VMEM((kind.NRP // 8 + 1, kind.W8, 2, 8, 128), i32),
         pltpu.VMEM((kind.N, 256), BF16),
         pltpu.VMEM((3, kind.SR, 128), F32),
-        pltpu.VMEM((3, kind.R2, 128), F32),
+        pltpu.VMEM((3, kind.SR, 128), F32),
     ]
 
 
@@ -573,7 +567,7 @@
         + kind_scratch(site)
         + [
             pltpu.VMEM((site.N, 384), BF16),
-            pltpu.VMEM((256, 256), BF16),
+            pltpu.VMEM((256, 128), BF16),
             pltpu.VMEM((STEPS, 2, 8, 128), F32),
             pltpu.VMEM((STEPS, 2, 8, 128), F32),
             pltpu.VMEM((STEPS, 8, 128), F32),

time: 66.1 us -> 60.4 us (0.914)
  the two profiles are of different devices: /device:TPU:511 before, /device:TPU:774 now
where the time goes in v2:
time: 60.4 us; the launch traced here: 60.1 us
  Pallas kernels  56.2 us (93%)
  local copies, waits for them, and re-layouts  2.6 us (4%)
  between operations  1.3 us (2%)
    pallas_call x1, Pallas kernels, shards(): pl.pallas_call(kernel, name='drm_window', out_shape=(jax.ShapeDtypeStruct...  56.2 us
    unnamed x4, local copies, waits for them, and re-layouts  2.6 us

profile of v2, /device:TPU:774, one launch (start us, length us, event | category | flops | bytes accessed | tf_op | source)
XLA Modules:
  0.0 60.1 jit_solution(11855336803023593167)
XLA Ops:
  1.3 56.2 %drm_window.1 = (f32[1,3,1,384]{3,2,1,0:T(1,128)}, f32[1,3,1,1536]{3,2,1,0:T(1,128)}) custom-call(f32[1,3,1,384]{3,2,1,0:T(1,128)} %bitcast.22, f32[1,3,1,384]{3,2,1,0:T(1,128)} %bitcast.23, f32[1,3,1,1536]{3,2,1,0:T(1,128)} %bitcast.16, f32[1,3,1,1536]{3,2,1,0:T(1,128)} %bitcast.17, s32[1,10,1,256]{3,2,1,0:T(1,128)} %bitcast.20, ...), custom_call_target="tpu_custom_call" | custom-call | tf_op jit(solution)/shard_map/drm_window/pallas_call | solution.py:556
  57.5 0.0 copy-start
  57.5 0.7 %copy-done = f32[1,3,1,384]{3,2,1,0:T(1,128)S(1)} copy-done((f32[1,3,1,384]{3,2,1,0:T(1,128)S(1)}, f32[1,3,1,384]{3,2,1,0:T(1,128)}, u32[]{:S(2)}) %copy-start) | copy-done | bytes 4632
  58.2 0.6 copy.28
  58.8 1.3 %copy.29 = f32[1,1,3,1536]{3,1,2,0:T(1,128)} copy(f32[1,1,3,1536]{3,1,2,0:T(1,128)} %bitcast.18) | data formatting | bytes 36864
Async XLA Ops:
  57.5 0.7 %copy-start = (f32[1,3,1,384]{3,2,1,0:T(1,128)S(1)}, f32[1,3,1,384]{3,2,1,0:T(1,128)}, u32[]{:S(2)}) copy-start(f32[1,3,1,384]{3,2,1,0:T(1,128)} %get-tuple-element.4) | copy-start | bytes 13828

commit v3 on v2

--- a/solution.py
+++ b/solution.py
@@ -176,16 +176,25 @@
         slot = keys & ((1 << SHIFT) - 1)
         plan_s[0, w * 8 : w * 8 + 8, :] = jnp.where(keys < BIG, slot >> 7, 1000)
         plan_s[1, w * 8 : w * 8 + 8, :] = slot & 127
-    targets = [((sub + v * 8) * 128 + lane + 1) << SHIFT for v in range(kind.NRP // 8)]
     sent = jnp.zeros((8, 128), jnp.int32)
     for side in range(2):
         wanted = spread(send_map[0, 0, side : side + 1, :])
         sent = jnp.where(sub == 2 * side, wanted + 1, sent)
         sent = jnp.where(sub == 2 * side + 1, wanted, sent)
-    targets.append(sent << SHIFT)
+    find_places(kind, [(kind.NRP // 8, sent << SHIFT)], key_s, pos_s)
+
+
+def setup_ends(kind, key_s, pos_s):
+    sub = iota2((8, 128), 0)
+    lane = iota2((8, 128), 1)
+    targets = [(v, ((sub + v * 8) * 128 + lane + 1) << SHIFT) for v in range(kind.NRP // 8)]
+    find_places(kind, targets, key_s, pos_s)
+
+
+def find_places(kind, targets, key_s, pos_s):
     for w in range(kind.W8):
         last = spread(key_s[w * 8 + 7 : w * 8 + 8, :])
-        for v, target in enumerate(targets):
+        for v, target in targets:
             column = jnp.zeros((8, 128), jnp.int32)
             for step in (64, 32, 16, 8, 4, 2, 1):
                 column = jnp.where(lane_take(last, column + (step - 1)) < target, column + step, column)
@@ -341,7 +350,7 @@
     reg_out, site_out,
     u_r, prev_r, f_r, tpad_r, d1_r, d2_r, node_r, key_r, plan_r, pos_r, hot_r, fe_r, cx_r, coef_r,
     u_s, prev_s, f_s, tpad_s, d1_s, d2_s, node_s, key_s, plan_s, pos_s, hot_s, fe_s, cx_s,
-    hot_l, scan, sends, recvs, layer_out, layer_in,
+    hot_l, scan, fills, sends, recvs, layer_out, layer_in,
     send_sem, recv_sem, layer_send_sem, layer_recv_sem,
 ):
     grp = lax.axis_index("grp")
@@ -381,13 +390,14 @@
                 recvs[n, side] = jnp.zeros((8, 128), F32)
 
     lane = iota2((8, 128), 1)
+    live = iota2((8, 128), 0) < 3
     greeted = has_lower.astype(jnp.int32) + has_upper.astype(jnp.int32) + jnp.where(is_site, 3, 1)
 
     def edge(n, side):
         peer = sub - 1 if side == 0 else sub + 1
         return pltpu.make_async_remote_copy(
-            src_ref=sends.at[n, side],
-            dst_ref=recvs.at[n, 1 - side],
+            src_ref=sends.at[n, side, 0:3],
+            dst_ref=recvs.at[n, 1 - side, 0:3],
             send_sem=send_sem.at[n, side],
             recv_sem=recv_sem.at[n, 1 - side],
             device_id=(grp, peer),
@@ -396,8 +406,8 @@
 
     def layer_copy(n, m):
         return pltpu.make_async_remote_copy(
-            src_ref=layer_out.at[n],
-            dst_ref=layer_in.at[n, m],
+            src_ref=layer_out.at[n, 0:3],
+            dst_ref=layer_in.at[n, m, 0:3],
             send_sem=layer_send_sem.at[n],
             recv_sem=layer_recv_sem.at[n, m],
             device_id=(target, sub),
@@ -406,12 +416,12 @@
 
     sides = ((has_lower, 0), (has_upper, 1))
 
-    def exchange(kind, n, pos, cx, fills):
+    def exchange(kind, n, pos, cx):
         found = read_ends(kind, kind.NRP // 8, pos, cx)
         for there, side in sides:
             for c in range(3):
                 force = found[c][2 * side : 2 * side + 1] - found[c][2 * side + 1 : 2 * side + 2]
-                sends[n, side, c : c + 1, :] = jnp.where(lane[0:1] < fills[side], force, 0.0)
+                sends[n, side, c : c + 1, :] = jnp.where(lane[0:1] < fills[side : side + 1, :], force, 0.0)
 
             @pl.when(there)
             def _():
@@ -423,6 +433,9 @@
             @pl.when(there)
             def _():
                 edge(n, 1 - side).wait_recv()
+
+    def arrived(n, side):
+        return jnp.where(live, recvs[n, side], 0.0)
 
     def finish(n, carry):
         for there, side in sides:
@@ -445,25 +458,32 @@
         coef_r[...] = jnp.zeros(coef_r.shape, F32)
         coef_r[:, :, 0 : kind.Q, :] = reg_coefs[0, 0]
         setup_plan(kind, reg_nodes, reg_send, node_r, key_r, plan_r, pos_r)
-        setup_hot(kind, [lambda i=i: reg_recv[0, 0, i : i + 1, :] for i in range(2)], hot_r)
         pl.semaphore_wait(barrier, greeted)
-        fills = (slot_fill[0, 0, 0], slot_fill[0, 0, 1])
+        for i in range(2):
+            fills[i : i + 1, :] = jnp.broadcast_to(slot_fill[0, :, i : i + 1], (1, 128))
+        fills[2:3, :] = jnp.broadcast_to(layer_fill[...], (1, 128))
 
         def step(n, carry):
             stiff_force(
                 kind, u_r, lambda a, b, k: coef_r[a, b, :, k * 128 : (k + 1) * 128],
                 node_r, plan_r, d1_r, d2_r, scan, fe_r, cx_r,
             )
-            exchange(kind, n, pos_r, cx_r, fills)
+            exchange(kind, n, pos_r, cx_r)
+
+            @pl.when(n == 0)
+            def _():
+                setup_ends(kind, key_r, pos_r)
+                setup_hot(kind, [lambda i=i: reg_recv[0, 0, i : i + 1, :] for i in range(2)], hot_r)
+
             node_forces(kind, pos_r, cx_r, f_r)
             minv = reg_minv[0]
             now = u_r[...]
             ahead = 2.0 * now - prev_r[...] + minv * f_r[...]
             prev_r[...] = now
             arrive(n)
-            u_r[...] = ahead + minv * drop(kind, [recvs[n, 0], recvs[n, 1]], hot_r)
+            u_r[...] = ahead + minv * drop(kind, [arrived(n, i) for i in range(2)], hot_r)
             found = pick(kind, u_r, layer_src[0])
-            layer_out[n] = jnp.where(lane < layer_fill[0, 0], found, 0.0)
+            layer_out[n] = jnp.where(lane < fills[2:3, :], found, 0.0)
             layer_copy(n, source).start()
             return carry
 
@@ -485,17 +505,23 @@
         f_s[...] = jnp.zeros(f_s.shape, F32)
         setup_tables(kind, site_table, True, tpad_s, d1_s, d2_s)
         setup_plan(kind, site_nodes, site_send, node_s, key_s, plan_s, pos_s)
-        setup_hot(kind, [lambda i=i: site_recv[0, 0, i : i + 1, :] for i in range(2)], hot_s)
-        setup_hot(kind, [lambda i=i: layer_dst[0, i] for i in range(3)], hot_l)
         pl.semaphore_wait(barrier, greeted)
-        fills = (slot_fill[0, 0, 2], slot_fill[0, 0, 3])
+        for i in range(2):
+            fills[i : i + 1, :] = jnp.broadcast_to(slot_fill[0, :, i + 2 : i + 3], (1, 128))
 
         def step(n, carry):
             stiff_force(
                 kind, u_s, lambda a, b, k: site_coefs[0, 0, a, b],
                 node_s, plan_s, d1_s, d2_s, scan, fe_s, cx_s,
             )
-            exchange(kind, n, pos_s, cx_s, fills)
+            exchange(kind, n, pos_s, cx_s)
+
+            @pl.when(n == 0)
+            def _():
+                setup_ends(kind, key_s, pos_s)
+                setup_hot(kind, [lambda i=i: site_recv[0, 0, i : i + 1, :] for i in range(2)], hot_s)
+                setup_hot(kind, [lambda i=i: layer_dst[0, i] for i in range(3)], hot_l)
+
             node_forces(kind, pos_s, cx_s, f_s)
             minv = site_minv[0]
             now = u_s[...]
@@ -504,10 +530,10 @@
             parts = []
             for m in range(3):
                 layer_copy(n, m).wait_recv()
-                parts.append(layer_in[n, m] * layer_stiff[0, m])
+                parts.append(jnp.where(live, layer_in[n, m], 0.0) * layer_stiff[0, m])
             ahead = ahead + minv * drop(kind, parts, hot_l)
             arrive(n)
-            u_s[...] = ahead + minv * drop(kind, [recvs[n, 0], recvs[n, 1]], hot_s)
+            u_s[...] = ahead + minv * drop(kind, [arrived(n, i) for i in range(2)], hot_s)
             return carry
 
         lax.fori_loop(0, STEPS, step, 0)
@@ -548,17 +574,14 @@
         args[i] = jnp.transpose(args[i], (0, 2, 1, 3))
     args[9] = args[9].T
     vmem = pl.BlockSpec(memory_space=pltpu.VMEM)
-    smem = pl.BlockSpec(memory_space=pltpu.SMEM)
     in_specs = [vmem] * len(args)
-    in_specs[16] = smem
-    in_specs[18] = smem
     kernel = functools.partial(body, reg, site, reg_groups, site_groups, lax.axis_size("sub"))
     outs = pl.pallas_call(
         kernel,
         name="drm_window",
         out_shape=(
-            jax.ShapeDtypeStruct((1, 3, 1, reg.N), F32),
-            jax.ShapeDtypeStruct((1, 3, 1, site.N), F32),
+            pltpu.VMEM((1, 3, 1, reg.N), F32),
+            pltpu.VMEM((1, 3, 1, site.N), F32),
         ),
         in_specs=in_specs,
         out_specs=(vmem, vmem),
@@ -568,6 +591,7 @@
         + [
             pltpu.VMEM((site.N, 384), BF16),
             pltpu.VMEM((256, 128), BF16),
+            pltpu.VMEM((8, 128), jnp.int32),
             pltpu.VMEM((STEPS, 2, 8, 128), F32),
             pltpu.VMEM((STEPS, 2, 8, 128), F32),
             pltpu.VMEM((STEPS, 8, 128), F32),

time: 60.4 us -> 58.2 us (0.964)
  local copies, waits for them, and re-layouts: 2.6 us -> 1.2 us
  Pallas kernels: 56.2 us -> 55.5 us
    unnamed x4 -> x2, local copies, waits for them, and re-layouts: 2.6 us -> 1.2 us
    pallas_call x1, Pallas kernels: 56.2 us -> 55.5 us  [shards(): pl.pallas_call(kernel, name='drm_window', out_shape=(pltpu.VMEM((1, 3, 1,...]
where the time goes in v3:
time: 58.2 us; the launch traced here: 58 us
  Pallas kernels  55.5 us (95%)
  between operations  1.29 us (2%)
  local copies, waits for them, and re-layouts  1.2 us (2%)
    pallas_call x1, Pallas kernels, shards(): pl.pallas_call(kernel, name='drm_window', out_shape=(pltpu.VMEM((1, 3, 1,...  55.5 us
    unnamed x2, local copies, waits for them, and re-layouts  1.2 us

profile of v3, /device:TPU:774, one launch (start us, length us, event | category | flops | bytes accessed | tf_op | source)
XLA Modules:
  0.0 58.0 jit_solution(7344388560404713954)
XLA Ops:
  1.3 55.5 %drm_window.1 = (f32[1,3,1,384]{3,2,1,0:T(1,128)S(1)}, f32[1,3,1,1536]{3,2,1,0:T(1,128)S(1)}) custom-call(f32[1,3,1,384]{3,2,1,0:T(1,128)} %bitcast.22, f32[1,3,1,384]{3,2,1,0:T(1,128)} %bitcast.23, f32[1,3,1,1536]{3,2,1,0:T(1,128)} %bitcast.18, f32[1,3,1,1536]{3,2,1,0:T(1,128)} %bitcast.19, s32[1,10,1,256]{3,2,1,0:T(1,128)} %bitcast.21, ...), custom_call_target="tpu_custom_call" | custom-call | tf_op jit(solution)/shard_map/drm_window/pallas_call | solution.py:579
  56.8 0.6 %copy.27 = f32[1,1,3,384]{3,1,2,0:T(1,128)} copy(f32[1,1,3,384]{3,1,2,0:T(1,128)S(1)} %bitcast.16) | data formatting | bytes 9216
  57.4 0.6 %copy.28 = f32[1,1,3,1536]{3,1,2,0:T(1,128)} copy(f32[1,1,3,1536]{3,1,2,0:T(1,128)S(1)} %bitcast.15) | data formatting | bytes 36864

commit v4 on v3

--- a/solution.py
+++ b/solution.py
@@ -218,20 +218,58 @@
         hot[:, k * 128 : (k + 1) * 128] = jnp.where(rows == load(), 1.0, 0.0).astype(BF16)
 
 
-def stiff_force(kind, u, coef, node_s, plan_s, d1, d2, scan, fe_s, cx_s):
+def gather_nodes(kind, u, node_s):
+    blocks = {}
+    for w in range(kind.W8):
+        index = node_s[w * 8 : w * 8 + 8, :]
+        found = gather_three(
+            index >> 7,
+            index & 127,
+            lambda c, r: u[c : c + 1, r * 128 : (r + 1) * 128],
+            range(kind.NR),
+        )
+        for c in range(3):
+            blocks[c, w] = found[c]
+    return blocks
+
+
+def setup_compact(kind, recv_map, minv, node_s, hot, equal, minv_c, slot_j):
+    rows = [recv_map[0, 0, i : i + 1, :] for i in range(2)]
+    wide = jnp.concatenate(rows, axis=1)
+    down = jnp.concatenate(
+        [jnp.broadcast_to(row.astype(F32), (128, 128)).T for row in rows], axis=0
+    ).astype(jnp.int32)
+    across = jnp.concatenate([down, down], axis=1) == wide
+    equal[...] = jnp.where(across, 1.0, 0.0).astype(BF16)
+    row = iota2((256, 256), 0)
+    col = iota2((256, 256), 1)
+    earlier = jnp.where(across & (row < col), 1.0, 0.0)
+    count = mm(jnp.ones((16, 256), F32), earlier)
+    name = jnp.where(count < 0.5, iota2((16, 256), 1) + 1, 0).astype(F32)
+    table = lax.dot_general(
+        name.astype(BF16), hot[...], (((1,), (1,)), ((), ())), preferred_element_type=F32
+    )
+    spread_minv = jnp.broadcast_to(minv, (8, kind.N))
+    for i in range(2):
+        minv_c[:, i * 128 : (i + 1) * 128] = pick(kind, spread_minv, rows[i])
+    for w in range(kind.W8):
+        index = node_s[w * 8 : w * 8 + 8, :]
+        idx_row, idx_lane = index >> 7, index & 127
+        found = jnp.zeros((8, 128), F32)
+        for r in range(kind.NR):
+            part = lane_take(spread(table[0:1, r * 128 : (r + 1) * 128]), idx_lane)
+            found = jnp.where(idx_row == r, part, found)
+        found = found.astype(jnp.int32) - 1
+        slot_j[0, w * 8 : w * 8 + 8, :] = jnp.where(found < 0, 1000, found >> 7)
+        slot_j[1, w * 8 : w * 8 + 8, :] = jnp.where(found < 0, 0, found & 127)
+
+
+def stiff_force(kind, values, coef, plan_s, d1, d2, scan, fe_s, cx_s):
     blocks = {}
     for k in range(kind.LC):
         for v in range(kind.PP // 8):
-            at = k * kind.PP + v * 8
-            index = node_s[at : at + 8, :]
-            found = gather_three(
-                index >> 7,
-                index & 127,
-                lambda c, r: u[c : c + 1, r * 128 : (r + 1) * 128],
-                range(kind.NR),
-            )
             for c in range(3):
-                blocks[c, k, v] = found[c]
+                blocks[c, k, v] = values[c, (k * kind.PP) // 8 + v]
     chunks = [(c, k) for c in range(3) for k in range(kind.LC)]
     cols = []
     for c, k in chunks:
@@ -350,7 +388,7 @@
     reg_out, site_out,
     u_r, prev_r, f_r, tpad_r, d1_r, d2_r, node_r, key_r, plan_r, pos_r, hot_r, fe_r, cx_r, coef_r,
     u_s, prev_s, f_s, tpad_s, d1_s, d2_s, node_s, key_s, plan_s, pos_s, hot_s, fe_s, cx_s,
-    hot_l, scan, fills, sends, recvs, layer_out, layer_in,
+    hot_l, kept, slot_c, equal, minv_c, small, scan, fills, sends, recvs, layer_out, layer_in,
     send_sem, recv_sem, layer_send_sem, layer_recv_sem,
 ):
     grp = lax.axis_index("grp")
@@ -465,8 +503,9 @@
 
         def step(n, carry):
             stiff_force(
-                kind, u_r, lambda a, b, k: coef_r[a, b, :, k * 128 : (k + 1) * 128],
-                node_r, plan_r, d1_r, d2_r, scan, fe_r, cx_r,
+                kind, gather_nodes(kind, u_r, node_r),
+                lambda a, b, k: coef_r[a, b, :, k * 128 : (k + 1) * 128],
+                plan_r, d1_r, d2_r, scan, fe_r, cx_r,
             )
             exchange(kind, n, pos_r, cx_r)
 
@@ -509,34 +548,69 @@
         for i in range(2):
             fills[i : i + 1, :] = jnp.broadcast_to(slot_fill[0, :, i + 2 : i + 3], (1, 128))
 
+        slot_c[...] = jnp.full(slot_c.shape, 1000, jnp.int32)
+        slot_c[1] = jnp.zeros(slot_c.shape[1:], jnp.int32)
+        small[...] = jnp.zeros(small.shape, F32)
+        hot_s[...] = jnp.zeros(hot_s.shape, BF16)
+
+        def keep_gathered(field):
+            for (c, w), block in gather_nodes(kind, field, node_s).items():
+                kept[c, w * 8 : w * 8 + 8, :] = block
+
+        def complete():
+            last = jnp.concatenate([small[0:8], small[8:16]], axis=0)
+            out = lax.dot_general(
+                last.astype(BF16), hot_s[...], (((1,), (1,)), ((), ())), preferred_element_type=F32
+            )
+            return u_s[...] + site_minv[0] * (out[0:8] + out[8:16])
+
+        keep_gathered(u_s)
+
         def step(n, carry):
+            values = {}
+            for w in range(kind.W8):
+                found = gather_three(
+                    slot_c[0, w * 8 : w * 8 + 8, :],
+                    slot_c[1, w * 8 : w * 8 + 8, :],
+                    lambda c, r: small[16 + c : 17 + c, r * 128 : (r + 1) * 128],
+                    range(2),
+                )
+                for c in range(3):
+                    values[c, w] = kept[c, w * 8 : w * 8 + 8, :] + found[c]
             stiff_force(
-                kind, u_s, lambda a, b, k: site_coefs[0, 0, a, b],
-                node_s, plan_s, d1_s, d2_s, scan, fe_s, cx_s,
+                kind, values, lambda a, b, k: site_coefs[0, 0, a, b],
+                plan_s, d1_s, d2_s, scan, fe_s, cx_s,
             )
             exchange(kind, n, pos_s, cx_s)
+            now = complete()
 
             @pl.when(n == 0)
             def _():
                 setup_ends(kind, key_s, pos_s)
                 setup_hot(kind, [lambda i=i: site_recv[0, 0, i : i + 1, :] for i in range(2)], hot_s)
                 setup_hot(kind, [lambda i=i: layer_dst[0, i] for i in range(3)], hot_l)
+                setup_compact(kind, site_recv, site_minv[0], node_s, hot_s, equal, minv_c, slot_c)
 
             node_forces(kind, pos_s, cx_s, f_s)
             minv = site_minv[0]
-            now = u_s[...]
             ahead = 2.0 * now - prev_s[...] + minv * f_s[...]
             prev_s[...] = now
             parts = []
             for m in range(3):
                 layer_copy(n, m).wait_recv()
                 parts.append(jnp.where(live, layer_in[n, m], 0.0) * layer_stiff[0, m])
-            ahead = ahead + minv * drop(kind, parts, hot_l)
+            u_s[...] = ahead + minv * drop(kind, parts, hot_l)
+            keep_gathered(u_s)
             arrive(n)
-            u_s[...] = ahead + minv * drop(kind, [arrived(n, i) for i in range(2)], hot_s)
+            hi, lo = split(jnp.concatenate([arrived(n, i) for i in range(2)], axis=1))
+            small[0:8] = hi
+            small[8:16] = lo
+            sums = mm(jnp.concatenate([hi, lo], axis=0), equal[...])
+            small[16:24] = (sums[0:8] + sums[8:16]) * minv_c[...]
             return carry
 
         lax.fori_loop(0, STEPS, step, 0)
+        u_s[...] = complete()
         for c in range(3):
             site_out[0, c] = u_s[c : c + 1, :]
         reg_out[...] = jnp.zeros(reg_out.shape, F32)
@@ -590,6 +664,11 @@
         + kind_scratch(site)
         + [
             pltpu.VMEM((site.N, 384), BF16),
+            pltpu.VMEM((3, site.SR, 128), F32),
+            pltpu.VMEM((2, site.SR, 128), jnp.int32),
+            pltpu.VMEM((256, 256), BF16),
+            pltpu.VMEM((8, 256), F32),
+            pltpu.VMEM((24, 256), F32),
             pltpu.VMEM((256, 128), BF16),
             pltpu.VMEM((8, 128), jnp.int32),
             pltpu.VMEM((STEPS, 2, 8, 128), F32),

time: 58.2 us -> 56.7 us (0.974)
  Pallas kernels: 55.5 us -> 54 us
    pallas_call x1, Pallas kernels: 55.5 us -> 54 us  [shards(): pl.pallas_call(kernel, name='drm_window', out_shape=(pltpu.VMEM((1, 3, 1,...]
where the time goes in v4:
time: 56.7 us; the launch traced here: 56.5 us
  Pallas kernels  54 us (95%)
  between operations  1.29 us (2%)
  local copies, waits for them, and re-layouts  1.2 us (2%)
    pallas_call x1, Pallas kernels, shards(): pl.pallas_call(kernel, name='drm_window', out_shape=(pltpu.VMEM((1, 3, 1,...  54 us
    unnamed x2, local copies, waits for them, and re-layouts  1.2 us

profile of v4, /device:TPU:774, one launch (start us, length us, event | category | flops | bytes accessed | tf_op | source)
XLA Modules:
  0.0 56.5 jit_solution(13711577936480135184)
XLA Ops:
  1.3 54.0 %drm_window.1 = (f32[1,3,1,384]{3,2,1,0:T(1,128)S(1)}, f32[1,3,1,1536]{3,2,1,0:T(1,128)S(1)}) custom-call(f32[1,3,1,384]{3,2,1,0:T(1,128)} %bitcast.22, f32[1,3,1,384]{3,2,1,0:T(1,128)} %bitcast.23, f32[1,3,1,1536]{3,2,1,0:T(1,128)} %bitcast.18, f32[1,3,1,1536]{3,2,1,0:T(1,128)} %bitcast.19, s32[1,10,1,256]{3,2,1,0:T(1,128)} %bitcast.21, ...), custom_call_target="tpu_custom_call" | custom-call | tf_op jit(solution)/shard_map/drm_window/pallas_call | solution.py:653
  55.3 0.6 %copy.27 = f32[1,1,3,384]{3,1,2,0:T(1,128)} copy(f32[1,1,3,384]{3,1,2,0:T(1,128)S(1)} %bitcast.16) | data formatting | bytes 9216
  55.9 0.6 %copy.28 = f32[1,1,3,1536]{3,1,2,0:T(1,128)} copy(f32[1,1,3,1536]{3,1,2,0:T(1,128)S(1)} %bitcast.15) | data formatting | bytes 36864

commit v5 on v4

--- a/solution.py
+++ b/solution.py
@@ -132,17 +132,11 @@
         prev[c : c + 1, :] = disp[0, c] - vel[0, c]
 
 
-def setup_tables(kind, table, flipped, tpad, d1, d2):
+def setup_tables(kind, table, tpad, d1, d2):
     tpad[...] = jnp.zeros(tpad.shape, F32)
-    if flipped:
-        tpad[0 : kind.P, 0 : kind.KQ] = table[...]
-        across = tpad[...]
-        whole = across.T
-    else:
-        for b in range(3):
-            tpad[b * kind.QP : b * kind.QP + kind.Q, 0 : kind.P] = table[b * kind.Q : (b + 1) * kind.Q, :]
-        whole = tpad[...]
-        across = whole.T
+    tpad[0 : kind.P, 0 : kind.KQ] = table[...]
+    across = tpad[...]
+    whole = across.T
     hi, lo = split(across[0 : kind.PP])
     stack = [hi, hi, lo]
     left = 128 - 3 * kind.PP
@@ -264,7 +258,44 @@
         slot_j[1, w * 8 : w * 8 + 8, :] = jnp.where(found < 0, 0, found & 127)
 
 
-def stiff_force(kind, values, coef, plan_s, d1, d2, scan, fe_s, cx_s):
+def setup_wide(kind, table, wide_1, wide_2):
+    for b in range(3):
+        for q in range(kind.Q):
+            entry = jnp.concatenate(
+                [table[b * kind.Q + q : b * kind.Q + q + 1, :], jnp.zeros((1, 128 - kind.P), F32)],
+                axis=1,
+            )
+            down = jnp.broadcast_to(entry, (128, 128)).T
+            wide_2[b * kind.Q + q] = -down[0 : kind.PP]
+    for p in range(kind.P):
+        for b in range(3):
+            for q in range(kind.Q):
+                wide_1[p, b * 8 + q : b * 8 + q + 1, :] = -wide_2[b * kind.Q + q, p : p + 1, :]
+
+
+def small_products(kind, values, coef, wide_1, wide_2, fe_s):
+    for k in range(kind.LC):
+        for c in range(3):
+            grad = [None] * 3
+            for p in range(kind.P):
+                block = values[c, (k * kind.PP + p) // 8]
+                row = jnp.broadcast_to(block[p % 8 : p % 8 + 1], (8, 128))
+                for b in range(3):
+                    term = wide_1[p, b * 8 : b * 8 + 8, :] * row
+                    grad[b] = term if p == 0 else grad[b] + term
+            terms = [None] * (kind.PP // 8)
+            for a in range(3):
+                flux = coef(a, 0, k) * grad[0] + coef(a, 1, k) * grad[1] + coef(a, 2, k) * grad[2]
+                for q in range(kind.Q):
+                    row = jnp.broadcast_to(flux[q : q + 1], (8, 128))
+                    for v in range(kind.PP // 8):
+                        term = wide_2[a * kind.Q + q, v * 8 : v * 8 + 8, :] * row
+                        terms[v] = term if a + q == 0 else terms[v] + term
+            for v in range(kind.PP // 8):
+                fe_s[c, k * kind.PP + v * 8 : k * kind.PP + v * 8 + 8, :] = terms[v]
+
+
+def large_products(kind, values, coef, d1, d2, fe_s):
     blocks = {}
     for k in range(kind.LC):
         for v in range(kind.PP // 8):
@@ -303,6 +334,9 @@
     fe = jnp.dot(d2[0 : kind.PP, :].astype(BF16), flux, preferred_element_type=F32)
     for i, (c, k) in enumerate(chunks):
         fe_s[c, k * kind.PP : (k + 1) * kind.PP, :] = fe[:, i * 128 : (i + 1) * 128]
+
+
+def sum_sorted(kind, plan_s, scan, fe_s, cx_s):
     sub = iota2((8, 128), 0)
     terms = {}
     both = []
@@ -386,7 +420,7 @@
     reg_table, site_table, reg_minv, site_minv, reg_send, reg_recv, site_send, site_recv,
     slot_fill, layer_src, layer_fill, layer_dst, layer_stiff,
     reg_out, site_out,
-    u_r, prev_r, f_r, tpad_r, d1_r, d2_r, node_r, key_r, plan_r, pos_r, hot_r, fe_r, cx_r, coef_r,
+    u_r, prev_r, f_r, wide_1, wide_2, node_r, key_r, plan_r, pos_r, hot_r, fe_r, cx_r, coef_r,
     u_s, prev_s, f_s, tpad_s, d1_s, d2_s, node_s, key_s, plan_s, pos_s, hot_s, fe_s, cx_s,
     hot_l, kept, slot_c, equal, minv_c, small, scan, fills, sends, recvs, layer_out, layer_in,
     send_sem, recv_sem, layer_send_sem, layer_recv_sem,
@@ -492,7 +526,8 @@
         kind = reg
         setup_state(kind, reg_disp, reg_vel, u_r, prev_r)
         f_r[...] = jnp.zeros(f_r.shape, F32)
-        setup_tables(kind, reg_table, False, tpad_r, d1_r, d2_r)
+        wide_1[...] = jnp.zeros(wide_1.shape, F32)
+        setup_wide(kind, reg_table, wide_1, wide_2)
         coef_r[...] = jnp.zeros(coef_r.shape, F32)
         coef_r[:, :, 0 : kind.Q, :] = reg_coefs[0, 0]
         setup_plan(kind, reg_nodes, reg_send, node_r, key_r, plan_r, pos_r)
@@ -502,11 +537,12 @@
         fills[2:3, :] = jnp.broadcast_to(layer_fill[...], (1, 128))
 
         def step(n, carry):
-            stiff_force(
+            small_products(
                 kind, gather_nodes(kind, u_r, node_r),
                 lambda a, b, k: coef_r[a, b, :, k * 128 : (k + 1) * 128],
-                plan_r, d1_r, d2_r, scan, fe_r, cx_r,
+                wide_1, wide_2, fe_r,
             )
+            sum_sorted(kind, plan_r, scan, fe_r, cx_r)
             exchange(kind, n, pos_r, cx_r)
 
             @pl.when(n == 0)
@@ -542,7 +578,7 @@
         kind = site
         setup_state(kind, site_disp, site_vel, u_s, prev_s)
         f_s[...] = jnp.zeros(f_s.shape, F32)
-        setup_tables(kind, site_table, True, tpad_s, d1_s, d2_s)
+        setup_tables(kind, site_table, tpad_s, d1_s, d2_s)
         setup_plan(kind, site_nodes, site_send, node_s, key_s, plan_s, pos_s)
         pl.semaphore_wait(barrier, greeted)
         for i in range(2):
@@ -577,10 +613,10 @@
                 )
                 for c in range(3):
                     values[c, w] = kept[c, w * 8 : w * 8 + 8, :] + found[c]
-            stiff_force(
-                kind, values, lambda a, b, k: site_coefs[0, 0, a, b],
-                plan_s, d1_s, d2_s, scan, fe_s, cx_s,
+            large_products(
+                kind, values, lambda a, b, k: site_coefs[0, 0, a, b], d1_s, d2_s, fe_s
             )
+            sum_sorted(kind, plan_s, scan, fe_s, cx_s)
             exchange(kind, n, pos_s, cx_s)
             now = complete()
 
@@ -617,16 +653,13 @@
         lax.fori_loop(0, STEPS, finish, 0)
 
 
-def kind_scratch(kind):
-    depth = pad_to(3 * kind.KQ, 128)
+def kind_scratch(kind, tables):
     i32 = jnp.int32
     return [
         pltpu.VMEM((8, kind.N), F32),
         pltpu.VMEM((8, kind.N), F32),
         pltpu.VMEM((8, kind.N), F32),
-        pltpu.VMEM((128, 128), F32),
-        pltpu.VMEM((128, 128), F32),
-        pltpu.VMEM((128, depth), F32),
+        *tables,
         pltpu.VMEM((kind.SR, 128), i32),
         pltpu.VMEM((kind.SR, 128), i32),
         pltpu.VMEM((2, kind.SR, 128), i32),
@@ -659,9 +692,22 @@
         ),
         in_specs=in_specs,
         out_specs=(vmem, vmem),
-        scratch_shapes=kind_scratch(reg)
+        scratch_shapes=kind_scratch(
+            reg,
+            [
+                pltpu.VMEM((reg.P, 24, 128), F32),
+                pltpu.VMEM((3 * reg.Q, reg.PP, 128), F32),
+            ],
+        )
         + [pltpu.VMEM((3, 3, reg.QP, reg.E), F32)]
-        + kind_scratch(site)
+        + kind_scratch(
+            site,
+            [
+                pltpu.VMEM((128, 128), F32),
+                pltpu.VMEM((128, 128), F32),
+                pltpu.VMEM((128, pad_to(3 * site.KQ, 128)), F32),
+            ],
+        )
         + [
             pltpu.VMEM((site.N, 384), BF16),
             pltpu.VMEM((3, site.SR, 128), F32),

time: 56.7 us -> 56.1 us (0.989)
  Pallas kernels: 54 us -> 53.4 us
    pallas_call x1, Pallas kernels: 54 us -> 53.4 us  [shards(): pl.pallas_call(kernel, name='drm_window', out_shape=(pltpu.VMEM((1, 3, 1,...]
where the time goes in v5:
time: 56.1 us; the launch traced here: 55.9 us
  Pallas kernels  53.4 us (95%)
  between operations  1.29 us (2%)
  local copies, waits for them, and re-layouts  1.2 us (2%)
    pallas_call x1, Pallas kernels, shards(): pl.pallas_call(kernel, name='drm_window', out_shape=(pltpu.VMEM((1, 3, 1,...  53.4 us
    unnamed x2, local copies, waits for them, and re-layouts  1.2 us

profile of v5, /device:TPU:774, one launch (start us, length us, event | category | flops | bytes accessed | tf_op | source)
XLA Modules:
  0.0 55.9 jit_solution(9630930599297159931)
XLA Ops:
  1.3 53.4 %drm_window.1 = (f32[1,3,1,384]{3,2,1,0:T(1,128)S(1)}, f32[1,3,1,1536]{3,2,1,0:T(1,128)S(1)}) custom-call(f32[1,3,1,384]{3,2,1,0:T(1,128)} %bitcast.22, f32[1,3,1,384]{3,2,1,0:T(1,128)} %bitcast.23, f32[1,3,1,1536]{3,2,1,0:T(1,128)} %bitcast.18, f32[1,3,1,1536]{3,2,1,0:T(1,128)} %bitcast.19, s32[1,10,1,256]{3,2,1,0:T(1,128)} %bitcast.21, ...), custom_call_target="tpu_custom_call" | custom-call | tf_op jit(solution)/shard_map/drm_window/pallas_call | solution.py:686
  54.7 0.6 %copy.27 = f32[1,1,3,384]{3,1,2,0:T(1,128)} copy(f32[1,1,3,384]{3,1,2,0:T(1,128)S(1)} %bitcast.16) | data formatting | bytes 9216
  55.3 0.6 %copy.28 = f32[1,1,3,1536]{3,1,2,0:T(1,128)} copy(f32[1,1,3,1536]{3,1,2,0:T(1,128)S(1)} %bitcast.15) | data formatting | bytes 36864

commit v6 on v5

--- a/solution.py
+++ b/solution.py
@@ -80,8 +80,27 @@
 
     total_bits = row_bits + 7
     for m in range(1, total_bits + 1):
-        for jb in range(m - 1, -1, -1):
+        jb = m
+        while jb > 0:
+            jb -= 1
             new = list(regs)
+            if jb - 1 >= row_bits:
+                far, near = 1 << (jb - row_bits), 1 << (jb - 1 - row_bits)
+                for v in range(count):
+                    x = regs[v]
+                    first = (bit_mask(jb, v) ^ bit_mask(m, v)) == 1
+                    second = (bit_mask(jb - 1, v) ^ bit_mask(m, v)) == 1
+                    other = lane_take(x, lane ^ far)
+                    mine = jnp.where(first, jnp.maximum(x, other), jnp.minimum(x, other))
+                    x = lane_take(regs[v], lane ^ near)
+                    other = lane_take(regs[v], lane ^ (far + near))
+                    theirs = jnp.where(first, jnp.maximum(x, other), jnp.minimum(x, other))
+                    new[v] = jnp.where(
+                        second, jnp.maximum(mine, theirs), jnp.minimum(mine, theirs)
+                    )
+                regs = new
+                jb -= 1
+                continue
             if 3 <= jb < row_bits:
                 step = 1 << (jb - 3)
                 for v in range(count):
@@ -190,8 +209,13 @@
         last = spread(key_s[w * 8 + 7 : w * 8 + 8, :])
         for v, target in targets:
             column = jnp.zeros((8, 128), jnp.int32)
-            for step in (64, 32, 16, 8, 4, 2, 1):
-                column = jnp.where(lane_take(last, column + (step - 1)) < target, column + step, column)
+            for step in (32, 8, 2):
+                passed = [
+                    jnp.where(lane_take(last, column + (i * step - 1)) < target, step, 0)
+                    for i in (1, 2, 3)
+                ]
+                column = column + passed[0] + passed[1] + passed[2]
+            column = jnp.where(lane_take(last, column) < target, column + 1, column)
             place = column * 8 - 1
             for r in range(8):
                 row = spread(key_s[w * 8 + r : w * 8 + r + 1, :])
@@ -636,7 +660,11 @@
                 layer_copy(n, m).wait_recv()
                 parts.append(jnp.where(live, layer_in[n, m], 0.0) * layer_stiff[0, m])
             u_s[...] = ahead + minv * drop(kind, parts, hot_l)
-            keep_gathered(u_s)
+
+            @pl.when(n < STEPS - 1)
+            def _():
+                keep_gathered(u_s)
+
             arrive(n)
             hi, lo = split(jnp.concatenate([arrived(n, i) for i in range(2)], axis=1))
             small[0:8] = hi

time: 56.1 us -> 56.2 us (level)
  no operation moved by 1% of the time
where the time goes in v6:
time: 56.2 us; the launch traced here: 56 us
  Pallas kernels  53.6 us (95%)
  between operations  1.29 us (2%)
  local copies, waits for them, and re-layouts  1.2 us (2%)
    pallas_call x1, Pallas kernels, shards(): pl.pallas_call(kernel, name='drm_window', out_shape=(pltpu.VMEM((1, 3, 1,...  53.6 us
    unnamed x2, local copies, waits for them, and re-layouts  1.2 us

profile of v6, /device:TPU:774, one launch (start us, length us, event | category | flops | bytes accessed | tf_op | source)
XLA Modules:
  0.0 56.0 jit_solution(549073448010458098)
XLA Ops:
  1.3 53.6 %drm_window.1 = (f32[1,3,1,384]{3,2,1,0:T(1,128)S(1)}, f32[1,3,1,1536]{3,2,1,0:T(1,128)S(1)}) custom-call(f32[1,3,1,384]{3,2,1,0:T(1,128)} %bitcast.22, f32[1,3,1,384]{3,2,1,0:T(1,128)} %bitcast.23, f32[1,3,1,1536]{3,2,1,0:T(1,128)} %bitcast.18, f32[1,3,1,1536]{3,2,1,0:T(1,128)} %bitcast.19, s32[1,10,1,256]{3,2,1,0:T(1,128)} %bitcast.21, ...), custom_call_target="tpu_custom_call" | custom-call | tf_op jit(solution)/shard_map/drm_window/pallas_call | solution.py:714
  54.8 0.6 %copy.27 = f32[1,1,3,384]{3,1,2,0:T(1,128)} copy(f32[1,1,3,384]{3,1,2,0:T(1,128)S(1)} %bitcast.16) | data formatting | bytes 9216
  55.4 0.6 %copy.28 = f32[1,1,3,1536]{3,1,2,0:T(1,128)} copy(f32[1,1,3,1536]{3,1,2,0:T(1,128)S(1)} %bitcast.15) | data formatting | bytes 36864

commit v7 on v6

--- a/solution.py
+++ b/solution.py
@@ -560,6 +560,11 @@
             fills[i : i + 1, :] = jnp.broadcast_to(slot_fill[0, :, i : i + 1], (1, 128))
         fills[2:3, :] = jnp.broadcast_to(layer_fill[...], (1, 128))
 
+        def send_layer(n):
+            found = pick(kind, u_r, layer_src[0])
+            layer_out[n] = jnp.where(lane < fills[2:3, :], found, 0.0)
+            layer_copy(n, source).start()
+
         def step(n, carry):
             small_products(
                 kind, gather_nodes(kind, u_r, node_r),
@@ -569,6 +574,10 @@
             sum_sorted(kind, plan_r, scan, fe_r, cx_r)
             exchange(kind, n, pos_r, cx_r)
 
+            @pl.when(n > 0)
+            def _():
+                send_layer(n - 1)
+
             @pl.when(n == 0)
             def _():
                 setup_ends(kind, key_r, pos_r)
@@ -581,12 +590,10 @@
             prev_r[...] = now
             arrive(n)
             u_r[...] = ahead + minv * drop(kind, [arrived(n, i) for i in range(2)], hot_r)
-            found = pick(kind, u_r, layer_src[0])
-            layer_out[n] = jnp.where(lane < fills[2:3, :], found, 0.0)
-            layer_copy(n, source).start()
             return carry
 
         lax.fori_loop(0, STEPS, step, 0)
+        send_layer(STEPS - 1)
         for c in range(3):
             reg_out[0, c] = u_r[c : c + 1, :]
         site_out[...] = jnp.zeros(site_out.shape, F32)

time: 56.2 us -> 56.7 us (level)
  no operation moved by 1% of the time
where the time goes in v7:
time: 56.7 us; the launch traced here: 56.6 us
  Pallas kernels  54.1 us (95%)
  between operations  1.29 us (2%)
  local copies, waits for them, and re-layouts  1.2 us (2%)
    pallas_call x1, Pallas kernels, shards(): pl.pallas_call(kernel, name='drm_window', out_shape=(pltpu.VMEM((1, 3, 1,...  54.1 us
    unnamed x2, local copies, waits for them, and re-layouts  1.2 us

profile of v7, /device:TPU:774, one launch (start us, length us, event | category | flops | bytes accessed | tf_op | source)
XLA Modules:
  0.0 56.6 jit_solution(13296107245184678634)
XLA Ops:
  1.3 54.1 %drm_window.1 = (f32[1,3,1,384]{3,2,1,0:T(1,128)S(1)}, f32[1,3,1,1536]{3,2,1,0:T(1,128)S(1)}) custom-call(f32[1,3,1,384]{3,2,1,0:T(1,128)} %bitcast.22, f32[1,3,1,384]{3,2,1,0:T(1,128)} %bitcast.23, f32[1,3,1,1536]{3,2,1,0:T(1,128)} %bitcast.18, f32[1,3,1,1536]{3,2,1,0:T(1,128)} %bitcast.19, s32[1,10,1,256]{3,2,1,0:T(1,128)} %bitcast.21, ...), custom_call_target="tpu_custom_call" | custom-call | tf_op jit(solution)/shard_map/drm_window/pallas_call | solution.py:721
  55.4 0.6 %copy.27 = f32[1,1,3,384]{3,1,2,0:T(1,128)} copy(f32[1,1,3,384]{3,1,2,0:T(1,128)S(1)} %bitcast.16) | data formatting | bytes 9216
  56.0 0.6 %copy.28 = f32[1,1,3,1536]{3,1,2,0:T(1,128)} copy(f32[1,1,3,1536]{3,1,2,0:T(1,128)S(1)} %bitcast.15) | data formatting | bytes 36864
